TPU v7x, 16 devices: a whole 2x2x2 slice. The times are simulated.
16 devices in a mesh: stage: 2 (over z), expert: 8 (over y, x, core).
Axes of the slice: x: 2, y: 2, z: 2, core: 2. Of those that a mesh axis runs over, the one named last changes fastest.
Arguments:
- x_acts: bfloat16 [2, 8192, 1024], P('stage', 'expert')
- expert_ids: int32 [2, 8192, 2], P('stage', 'expert')
- gate_vals: float32 [2, 8192, 2], P('stage', 'expert')
- w_gate: bfloat16 [2, 8, 1024, 1536], P('stage', 'expert')
- w_up: bfloat16 [2, 8, 1024, 1536], P('stage', 'expert')
- w_down: bfloat16 [2, 8, 1536, 1024], P('stage', 'expert')
- grad_out: bfloat16 [2, 8192, 1024], P('stage', 'expert')
Outputs:
- output 1: bfloat16 [2, 8192, 1024], P('stage', 'expert')
- output 2: bfloat16 [2, 8192, 1024], P('stage', 'expert')
- output 3: bfloat16 [2, 8, 1024, 1536], P('stage', 'expert')
- output 4: bfloat16 [2, 8, 1024, 1536], P('stage', 'expert')
- output 5: bfloat16 [2, 8, 1536, 1024], P('stage', 'expert')
All inputs are finite; a program needn't handle non-finite values.
Results may differ from a plain program's by a relative error of at most 0.00856692.
Values are sent between devices in bfloat16 or wider.
A program may use at most 1 GiB of HBM per device.

v0:
```python
import jax
import jax.numpy as jnp
from jax import lax
from jax.sharding import PartitionSpec as P


def plan_rows(expert_ids, gate_vals, local_experts, ep_size, capacity):
    tok_dev, top_k = expert_ids.shape
    experts = local_experts * ep_size
    flat_ids = expert_ids.reshape(-1)
    one_hot = (flat_ids[:, None] == jnp.arange(experts)[None, :]).astype(jnp.int32)
    ranks = jnp.cumsum(one_hot, axis=0) - 1
    positions = jnp.sum(ranks * one_hot, axis=1)
    slots = ((flat_ids % local_experts) * ep_size + flat_ids // local_experts) * capacity + positions
    row_count = experts * capacity
    tok_of_choice = jnp.arange(tok_dev * top_k, dtype=jnp.int32) // top_k
    row_token = jax.ops.segment_sum(tok_of_choice + 1, slots, num_segments=row_count) - 1
    row_gate = jax.ops.segment_sum(gate_vals.reshape(-1), slots, num_segments=row_count)
    return slots.reshape(tok_dev, top_k), row_token, row_gate


def expert_forward(x_rows, wg_loc, wu_loc, wd_loc):
    pre_gate = jnp.einsum('epcd,edf->epcf', x_rows, wg_loc, preferred_element_type=jnp.float32)
    pre_up = jnp.einsum('epcd,edf->epcf', x_rows, wu_loc, preferred_element_type=jnp.float32)
    sig_gate = jax.nn.sigmoid(pre_gate)
    act_gate = pre_gate * sig_gate
    hidden = (act_gate * pre_up).astype(jnp.bfloat16)
    out_rows = jnp.einsum('epcf,efd->epcd', hidden, wd_loc, preferred_element_type=jnp.float32).astype(jnp.bfloat16)
    return out_rows, (pre_gate, pre_up, sig_gate, act_gate, hidden)


def expert_backward(x_rows, do_rows, fwd_saved, wg_loc, wu_loc, wd_loc):
    pre_gate, pre_up, sig_gate, act_gate, hidden = fwd_saved
    g_hidden = jnp.einsum('epcd,efd->epcf', do_rows, wd_loc, preferred_element_type=jnp.float32)
    g_up = (g_hidden * act_gate).astype(jnp.bfloat16)
    g_pre = (g_hidden * pre_up * sig_gate * (1.0 + pre_gate * (1.0 - sig_gate))).astype(jnp.bfloat16)
    dx_rows = (jnp.einsum('epcf,edf->epcd', g_pre, wg_loc, preferred_element_type=jnp.float32) + jnp.einsum('epcf,edf->epcd', g_up, wu_loc, preferred_element_type=jnp.float32)).astype(jnp.bfloat16)
    g_wgate = jnp.einsum('epcd,epcf->edf', x_rows, g_pre, preferred_element_type=jnp.float32).astype(jnp.bfloat16)
    g_wup = jnp.einsum('epcd,epcf->edf', x_rows, g_up, preferred_element_type=jnp.float32).astype(jnp.bfloat16)
    g_wdown = jnp.einsum('epcf,epcd->efd', hidden, do_rows, preferred_element_type=jnp.float32).astype(jnp.bfloat16)
    return dx_rows, g_wgate, g_wup, g_wdown


def gather_choices(rows_flat, slots):
    picked = jnp.take(rows_flat, slots.reshape(-1), axis=0)
    return picked.reshape(slots.shape[0], slots.shape[1], rows_flat.shape[1])


def solution(mesh):
    stages = mesh.shape['stage']
    ep_size = mesh.shape['expert']
    send_next = [(src_stage, (src_stage + 1) % stages) for src_stage in range(stages)]
    send_prev = [((src_stage + 1) % stages, src_stage) for src_stage in range(stages)]
    tok_spec = P('stage', 'expert', None)
    w_spec = P('stage', 'expert', None, None)

    def device_fn(x_acts, expert_ids, gate_vals, w_gate, w_up, w_down, grad_out):
        x_mine = lax.ppermute(x_acts[0], 'stage', send_next)
        ids_mine = lax.ppermute(expert_ids[0], 'stage', send_next)
        gate_mine = lax.ppermute(gate_vals[0], 'stage', send_next)
        tok_dev, top_k = ids_mine.shape
        model_dim = x_mine.shape[1]
        local_experts = w_gate.shape[1]
        capacity = 2 * tok_dev * top_k // (local_experts * ep_size) + 1
        slots, row_token, row_gate = plan_rows(ids_mine, gate_mine, local_experts, ep_size, capacity)
        safe_token = jnp.maximum(row_token, 0)
        buf_shape = (local_experts, ep_size, capacity, model_dim)
        x_send = jnp.where((row_token >= 0)[:, None], jnp.take(x_mine, safe_token, axis=0), jnp.zeros((), jnp.bfloat16)).reshape(buf_shape)
        x_rows = lax.all_to_all(x_send, 'expert', 1, 1, tiled=True)
        out_rows, fwd_saved = expert_forward(x_rows, w_gate[0], w_up[0], w_down[0])
        out_back = lax.all_to_all(out_rows, 'expert', 1, 1, tiled=True).reshape(-1, model_dim)
        picked = gather_choices(out_back, slots)
        moe_out = jnp.sum(gate_mine[:, :, None] * picked.astype(jnp.float32), axis=1).astype(jnp.bfloat16)
        do_send = (row_gate[:, None] * jnp.take(grad_out[0], safe_token, axis=0).astype(jnp.float32)).astype(jnp.bfloat16).reshape(buf_shape)
        do_rows = lax.all_to_all(do_send, 'expert', 1, 1, tiled=True)
        dx_rows, g_wgate, g_wup, g_wdown = expert_backward(x_rows, do_rows, fwd_saved, w_gate[0], w_up[0], w_down[0])
        dx_back = lax.all_to_all(dx_rows, 'expert', 1, 1, tiled=True).reshape(-1, model_dim)
        grad_in = jnp.sum(gather_choices(dx_back, slots).astype(jnp.float32), axis=1).astype(jnp.bfloat16)
        grad_x = lax.ppermute(grad_in, 'stage', send_prev)
        return moe_out[None], grad_x[None], g_wgate[None], g_wup[None], g_wdown[None]

    return jax.shard_map(device_fn, mesh=mesh, in_specs=(tok_spec, tok_spec, tok_spec, w_spec, w_spec, w_spec, tok_spec), out_specs=(tok_spec, tok_spec, w_spec, w_spec, w_spec), check_vma=False)
```

profile of v0, /device:TPU:1, one launch (start us, length us, event | category | flops | bytes accessed | tf_op | source)
XLA Modules:
  0.0 692.2 jit_solution(14677399855968945512)
XLA Ops:
  0.6 0.0 copy-start
  0.6 2.2 collective-permute-start.2
  2.8 0.1 collective-permute-start.1
  2.9 45.6 %collective-permute-done.1 = s32[1024,2]{0,1:T(2,128)S(1)} collective-permute-done((s32[1024,2]{0,1:T(2,128)}, s32[1024,2]{0,1:T(2,128)S(1)}, u32[]{:S(2)}, u32[]{:S(2)}) %collective-permute-start.1) | collective-permute-done | bytes 8224 | tf_op jit(solution)/shard_map/ppermute | solution.py:59
  48.4 1.0 copy.19
  49.4 1.3 eq.27
  50.8 0.0 copy-start.1
  50.8 1.3 eq.31
  52.1 2.3 reduce-window.6
  54.4 0.3 slice_reduce_fusion
  54.7 0.2 reduce-window.9
  54.8 1.0 copy.21
  55.9 1.4 mul.75
  57.2 0.1 add_bitcast_fusion
  57.4 0.0 copy-start.3
  57.4 0.6 copy-done.3
  58.0 11.2 %scatter_custom_fusion = s32[4104]{0:T(1024)S(1)} fusion(s32[2048]{0:T(1024)S(1)} %bitcast.120, s32[2048]{0:T(1024)S(1)} %fusion.43, s32[]{:T(128)} %constant.75.clone.1), kind=kCustom, calls=%fused_computation.64 | custom fusion | flops 2048 | bytes 16420 | tf_op jit(solution)/shard_map/scatter-add | solution.py:17
  69.3 0.0 collective-permute-done.2
  69.3 21.3 %gather_fusion = bf16[4104,1024]{1,0:T(8,128)(2,1)} fusion(bf16[1024,1024]{1,0:T(8,128)(2,1)} %collective-permute-done.2, s32[5120]{0:T(1024)S(1)} %pad_clamp_fusion), kind=kCustom, calls=%fused_computation.clone | custom fusion | bytes 16826400 | tf_op jit(solution)/shard_map/jit(_take)/gather | solution.py:68
  90.6 0.0 copy-done.1
  90.6 8.4 %select_select_fusion = bf16[4104,1024]{1,0:T(8,128)(2,1)} fusion(bf16[4104,1024]{1,0:T(8,128)(2,1)} %gather_fusion, pred[4104]{0:T(1024)(128)(4,1)S(1)} %get-tuple-element.11, pred[4104]{0:T(1024)(128)(4,1)S(1)} %get-tuple-element.10), kind=kLoop, calls=%fused_computation.27 | loop fusion | flops 8404992 | bytes 16818192 | tf_op jit(solution)/shard_map/jit(_where)/select_n | solution.py:68
  99.0 9.1 %reshape.167 = bf16[1,8,513,1024]{3,2,1,0:T(8,128)(2,1)} reshape(bf16[4104,1024]{1,0:T(8,128)(2,1)} %select_select_fusion) | data formatting | bytes 16809984 | tf_op jit(solution)/shard_map/reshape | solution.py:68
  108.1 6.1 all-to-all-start
  114.2 0.0 copy-done.6
  114.2 1.5 collective-permute-start
  115.7 1.4 collective-permute-done
  117.1 1.0 copy.18
  118.1 1.3 reshape.223
  119.4 21.3 %gather_fusion.2 = bf16[4104,1024]{1,0:T(8,128)(2,1)} fusion(bf16[1024,1024]{1,0:T(8,128)(2,1)} %bitcast.114, s32[5120]{0:T(1024)S(1)} %pad_clamp_fusion), kind=kCustom, calls=%fused_computation.2.clone | custom fusion | bytes 16826400 | tf_op jit(solution)/shard_map/jit(_take)/gather | solution.py:74
  140.7 11.4 %scatter_custom_fusion.1 = f32[4104]{0:T(1024)S(1)} fusion(s32[2048]{0:T(1024)S(1)} %bitcast.121, f32[2048]{0:T(1024)S(1)} %reshape.223, f32[]{:T(128)} %constant.81.clone.1), kind=kCustom, calls=%fused_computation.60 | custom fusion | flops 2048 | bytes 16420 | tf_op jit(solution)/shard_map/scatter-add | solution.py:18
  152.2 8.2 %multiply_convert_fusion.3 = bf16[4104,1024]{1,0:T(8,128)(2,1)} fusion(bf16[4104,1024]{1,0:T(8,128)(2,1)} %gather_fusion.2, f32[4104]{0:T(1024)S(1)} %scatter_custom_fusion.1, pred[4104]{0:T(1024)(128)(4,1)S(1)} %get-tuple-element.11), kind=kLoop, calls=%fused_computation.12 | loop fusion | flops 16809984 | bytes 16830504 | tf_op jit(solution)/shard_map/convert_element_type | solution.py:74
  160.3 9.1 %reshape.174 = bf16[1,8,513,1024]{3,2,1,0:T(8,128)(2,1)} reshape(bf16[4104,1024]{1,0:T(8,128)(2,1)} %multiply_convert_fusion.3) | data formatting | bytes 16809984 | tf_op jit(solution)/shard_map/reshape | solution.py:74
  169.5 36.4 %all-to-all-done = bf16[1,8,513,1024]{3,2,0,1:T(8,128)(2,1)} async-done(((bf16[1,8,513,1024]{3,2,0,1:T(8,128)(2,1)}), bf16[1,8,513,1024]{3,2,0,1:T(8,128)(2,1)}, u32[]{:S(2)}, u32[]{:S(2)}) %all-to-all-start) | async-done | bytes 8405024 | tf_op jit(solution)/shard_map/all_to_all | solution.py:69
  205.9 8.7 %all-to-all-start.2 = ((bf16[1,8,513,1024]{3,2,0,1:T(8,128)(2,1)}), bf16[1,8,513,1024]{3,2,0,1:T(8,128)(2,1)}, u32[]{:S(2)}, u32[]{:S(2)}) async-start(bf16[1,8,513,1024]{3,2,0,1:T(8,128)(2,1)} %bitcast.116), calls=%async_computation.2 | async-start | bytes 17039360 | tf_op jit(solution)/shard_map/all_to_all | solution.py:75
  214.6 21.6 %fusion.10 = f32[8,513,1536]{2,1,0:T(8,128)} fusion(bf16[1,8,513,1024]{3,2,0,1:T(8,128)(2,1)} %all-to-all-done, bf16[1,1,1024,1536]{3,2,1,0:T(8,128)(2,1)} %param.15), kind=kOutput, calls=%fused_computation.22 | convolution fusion | flops 12910067712 | bytes 36765696 | tf_op jit(solution)/shard_map/epcd,edf->epcf/dot_general | solution.py:24
  236.2 0.0 copy-done.5
  236.2 20.6 %fusion.12 = f32[8,513,1536]{2,1,0:T(8,128)} fusion(bf16[1,8,513,1024]{3,2,0,1:T(8,128)(2,1)} %all-to-all-done, bf16[1,1,1024,1536]{3,2,1,0:T(8,128)(2,1)S(1)} %copy-done.5), kind=kOutput, calls=%fused_computation.24 | convolution fusion | flops 12910067712 | bytes 36765696 | tf_op jit(solution)/shard_map/epcd,edf->epcf/dot_general | solution.py:23
  256.8 49.5 %all-to-all-done.2 = bf16[1,8,513,1024]{3,2,0,1:T(8,128)(2,1)} async-done(((bf16[1,8,513,1024]{3,2,0,1:T(8,128)(2,1)}), bf16[1,8,513,1024]{3,2,0,1:T(8,128)(2,1)}, u32[]{:S(2)}, u32[]{:S(2)}) %all-to-all-start.2) | async-done | bytes 8405024 | tf_op jit(solution)/shard_map/all_to_all | solution.py:75
  306.3 0.0 copy-done
  306.3 40.4 %multiply_convert_fusion = (bf16[8,513,1536]{2,1,0:T(8,128)(2,1)}, bf16[8,513,1536]{2,1,0:T(8,128)(2,1)}, bf16[8,513,1536]{2,1,0:T(8,128)(2,1)}) fusion(f32[8,513,1536]{2,1,0:T(8,128)} %fusion.12, f32[8,513,1536]{2,1,0:T(8,128)} %fusion.10, bf16[1,1,1536,1024]{3,2,1,0:T(8,128)(2,1)S(1)} %copy-done, bf16[1,8,513,1024]{3,2,0,1:T(8,128)(2,1)} %all-to-all-done.2), kind=kOutput, calls=%fused_computation.6 | convolution fusion | flops 13004623872 | bytes 99803136 | tf_op jit(solution)/shard_map/epcd,efd->epcf/dot_general | solution.py:34
  346.7 19.7 %fusion.31 = f32[8,513,1024]{2,1,0:T(8,128)} fusion(bf16[8,513,1536]{2,1,0:T(8,128)(2,1)} %get-tuple-element.8, bf16[1,1,1024,1536]{3,2,1,0:T(8,128)(2,1)} %param.14), kind=kOutput, calls=%fused_computation.39 | convolution fusion | flops 12910067712 | bytes 32563200 | tf_op jit(solution)/shard_map/epcf,edf->epcd/dot_general | solution.py:37
  366.4 23.8 %fusion.1 = bf16[1,8,513,1024]{3,2,0,1:T(8,128)(2,1)} fusion(f32[8,513,1024]{2,1,0:T(8,128)} %fusion.31, bf16[8,513,1536]{2,1,0:T(8,128)(2,1)} %get-tuple-element.7, bf16[1,1,1024,1536]{3,2,1,0:T(8,128)(2,1)} %param.15), kind=kOutput, calls=%fused_computation.13 | convolution fusion | flops 12918472704 | bytes 40968192 | tf_op jit(solution)/shard_map/epcf,edf->epcd/dot_general | solution.py:37
  390.1 9.2 %all-to-all-start.3 = ((bf16[1,8,513,1024]{3,2,0,1:T(8,128)(2,1)}), bf16[1,8,513,1024]{3,2,0,1:T(8,128)(2,1)}, u32[]{:S(2)}, u32[]{:S(2)}) async-start(bf16[1,8,513,1024]{3,2,0,1:T(8,128)(2,1)} %fusion.1), calls=%async_computation.3 | async-start | bytes 17039360 | tf_op jit(solution)/shard_map/all_to_all | solution.py:77
  399.3 18.5 %convert_bitcast_fusion = bf16[1,8,513,1024]{3,2,0,1:T(8,128)(2,1)} fusion(bf16[8,513,1536]{2,1,0:T(8,128)(2,1)} %get-tuple-element.9, bf16[1,1,1536,1024]{3,2,1,0:T(8,128)(2,1)S(1)} %copy-done), kind=kOutput, calls=%fused_computation.26 | convolution fusion | flops 12914270208 | bytes 24158208 | tf_op jit(solution)/shard_map/epcf,efd->epcd/dot_general | solution.py:28
  417.9 73.1 %all-to-all-done.3 = bf16[1,8,513,1024]{3,2,0,1:T(8,128)(2,1)} async-done(((bf16[1,8,513,1024]{3,2,0,1:T(8,128)(2,1)}), bf16[1,8,513,1024]{3,2,0,1:T(8,128)(2,1)}, u32[]{:S(2)}, u32[]{:S(2)}) %all-to-all-start.3) | async-done | bytes 8405024 | tf_op jit(solution)/shard_map/all_to_all | solution.py:77
  491.0 8.9 %all-to-all-start.1 = ((bf16[1,8,513,1024]{3,2,0,1:T(8,128)(2,1)}), bf16[1,8,513,1024]{3,2,0,1:T(8,128)(2,1)}, u32[]{:S(2)}, u32[]{:S(2)}) async-start(bf16[1,8,513,1024]{3,2,0,1:T(8,128)(2,1)} %convert_bitcast_fusion), calls=%async_computation.1 | async-start | bytes 17039360 | tf_op jit(solution)/shard_map/all_to_all | solution.py:71
  499.9 0.0 copy-done.2
  499.9 0.0 copy-done.4
  499.9 20.1 %fusion.23 = bf16[1,1,1024,1536]{3,2,1,0:T(8,128)(2,1)} fusion(bf16[8,513,1536]{2,1,0:T(8,128)(2,1)} %get-tuple-element.7, bf16[1,8,513,1024]{3,2,0,1:T(8,128)(2,1)} %all-to-all-done), kind=kOutput, calls=%fused_computation.35 | convolution fusion | flops 12911640576 | bytes 24158208 | tf_op jit(solution)/shard_map/epcd,epcf->edf/dot_general | solution.py:39
  520.1 20.1 %fusion.26 = bf16[1,1,1536,1024]{3,2,1,0:T(8,128)(2,1)} fusion(bf16[8,513,1536]{2,1,0:T(8,128)(2,1)} %get-tuple-element.9, bf16[1,8,513,1024]{3,2,0,1:T(8,128)(2,1)} %all-to-all-done.2), kind=kOutput, calls=%fused_computation.36 | convolution fusion | flops 12911640576 | bytes 24158208 | tf_op jit(solution)/shard_map/epcf,epcd->efd/dot_general | solution.py:40
  540.1 9.1 %reshape.176 = bf16[4104,1024]{1,0:T(8,128)(2,1)} reshape(bf16[1,8,513,1024]{3,2,0,1:T(8,128)(2,1)} %all-to-all-done.3) | data formatting | bytes 16809984 | tf_op jit(solution)/shard_map/reshape | solution.py:77
  549.3 15.6 %gather_fusion.3 = bf16[2048,1024]{1,0:T(8,128)(2,1)} fusion(bf16[4104,1024]{1,0:T(8,128)(2,1)} %reshape.176, s32[2048]{0:T(1024)S(1)} %broadcast_clamp_fusion), kind=kCustom, calls=%fused_computation.3.clone | custom fusion | bytes 8396800 | tf_op jit(solution)/shard_map/jit(_take)/gather | solution.py:45
  564.9 26.6 %all-to-all-done.1 = bf16[1,8,513,1024]{3,2,0,1:T(8,128)(2,1)} async-done(((bf16[1,8,513,1024]{3,2,0,1:T(8,128)(2,1)}), bf16[1,8,513,1024]{3,2,0,1:T(8,128)(2,1)}, u32[]{:S(2)}, u32[]{:S(2)}) %all-to-all-start.1) | async-done | bytes 8405024 | tf_op jit(solution)/shard_map/all_to_all | solution.py:71
  591.5 9.1 %reshape.172 = bf16[4104,1024]{1,0:T(8,128)(2,1)} reshape(bf16[1,8,513,1024]{3,2,0,1:T(8,128)(2,1)} %all-to-all-done.1) | data formatting | bytes 16809984 | tf_op jit(solution)/shard_map/reshape | solution.py:71
  600.7 15.5 %gather_fusion.1 = bf16[2048,1024]{1,0:T(8,128)(2,1)} fusion(bf16[4104,1024]{1,0:T(8,128)(2,1)} %reshape.172, s32[2048]{0:T(1024)S(1)} %broadcast_clamp_fusion), kind=kCustom, calls=%fused_computation.1.clone | custom fusion | bytes 8396800 | tf_op jit(solution)/shard_map/jit(_take)/gather | solution.py:45
  616.1 7.2 %broadcast_select_fusion = (bf16[2048,1024]{1,0:T(8,128)(2,1)}, f32[2048,1024]{1,0:T(8,128)}) fusion(bf16[2048,1024]{1,0:T(8,128)(2,1)} %gather_fusion.3, pred[2048]{0:T(1024)(128)(4,1)S(1)} %compare_and_fusion, bf16[2048,1024]{1,0:T(8,128)(2,1)} %gather_fusion.1), kind=kLoop, calls=%fused_computation.33 | loop fusion | flops 6291456 | bytes 20973568 | tf_op jit(solution)/shard_map/jit(_take)/select_n | solution.py:45
  623.4 7.2 %reshape.177 = bf16[1024,2,1024]{2,1,0:T(2,128)(2,1)} reshape(bf16[2048,1024]{1,0:T(8,128)(2,1)} %get-tuple-element.12) | data formatting | bytes 8388608 | tf_op jit(solution)/shard_map/reshape | solution.py:46
  630.6 12.7 %reduce_sum.35 = bf16[1024,1024]{1,0:T(8,128)(2,1)} reduce(bf16[1024,2,1024]{2,1,0:T(2,128)(2,1)} %reshape.177, bf16[]{:T(256)} %constant.79.clone.1), dimensions={1}, to_apply=%region_6.9 | reduce | flops 1048576 | bytes 6291458 | tf_op jit(solution)/shard_map/reduce_sum | solution.py:78
  643.3 1.5 collective-permute-start.3
  644.7 20.1 %fusion.20 = bf16[1,1,1024,1536]{3,2,1,0:T(8,128)(2,1)} fusion(bf16[8,513,1536]{2,1,0:T(8,128)(2,1)} %get-tuple-element.8, bf16[1,8,513,1024]{3,2,0,1:T(8,128)(2,1)} %all-to-all-done), kind=kOutput, calls=%fused_computation.34 | convolution fusion | flops 12911640576 | bytes 24158208 | tf_op jit(solution)/shard_map/epcd,epcf->edf/dot_general | solution.py:38
  664.8 10.6 %reshape.178 = f32[1024,2,1024]{2,1,0:T(2,128)} reshape(f32[2048,1024]{1,0:T(8,128)} %get-tuple-element.13) | data formatting | bytes 16777216 | tf_op jit(solution)/shard_map/convert_element_type | solution.py:73
  675.4 13.5 %multiply_reduce_fusion = bf16[1024,1024]{1,0:T(8,128)(2,1)} fusion(f32[1024,2,1024]{2,1,0:T(2,128)} %reshape.178, f32[1024,2]{1,0:T(8,128)} %copy.18), kind=kLoop, calls=%fused_computation.28 | loop fusion | flops 3145728 | bytes 10493952 | tf_op jit(solution)/shard_map/reduce_sum | solution.py:73
  688.9 0.0 collective-permute-done.3
  688.9 3.1 copy.30
  (14 shorter events, 0.1 us)
Async XLA Ops:
  0.6 305.6 %copy-start = (bf16[1,1,1536,1024]{3,2,1,0:T(8,128)(2,1)S(1)}, bf16[1,1,1536,1024]{3,2,1,0:T(8,128)(2,1)}, u32[]{:S(2)}) copy-start(bf16[1,1,1536,1024]{3,2,1,0:T(8,128)(2,1)} %param.16) | copy-start | bytes 9437188
  0.6 68.6 %collective-permute-start.2 = (bf16[1024,1024]{1,0:T(8,128)(2,1)}, bf16[1024,1024]{1,0:T(8,128)(2,1)}, u32[]{:S(2)}, u32[]{:S(2)}) collective-permute-start(bf16[1024,1024]{1,0:T(8,128)(2,1)} %bitcast.122), channel_id=1, source_target_pairs={{0,8},{8,0},{1,9},{9,1},{2,10},{10,2},{3,11},{11,3},{4,12},{12,4},... | collective-permute-start | bytes 6291464 | tf_op jit(solution)/shard_map/ppermute | solution.py:58
  2.8 45.6 %collective-permute-start.1 = (s32[1024,2]{0,1:T(2,128)}, s32[1024,2]{0,1:T(2,128)S(1)}, u32[]{:S(2)}, u32[]{:S(2)}) collective-permute-start(s32[1024,2]{0,1:T(2,128)} %bitcast.123), channel_id=1, source_target_pairs={{0,8},{8,0},{1,9},{9,1},{2,10},{10,2},{3,11},{11,3},{4,12},{12,4},... | collective-permute-start | bytes 24584 | tf_op jit(solution)/shard_map/ppermute | solution.py:59
  50.8 39.8 %copy-start.1 = (s32[2048]{0:T(1024)}, s32[2048]{0:T(1024)S(1)}, u32[]{:S(2)}) copy-start(s32[2048]{0:T(1024)S(1)} %eq.27) | copy-start | bytes 24580
  57.4 0.6 copy-start.3
  108.1 6.1 copy-start.6
  108.1 97.8 %all-to-all-start = ((bf16[1,8,513,1024]{3,2,0,1:T(8,128)(2,1)}), bf16[1,8,513,1024]{3,2,0,1:T(8,128)(2,1)}, u32[]{:S(2)}, u32[]{:S(2)}) async-start(bf16[1,8,513,1024]{3,2,0,1:T(8,128)(2,1)} %bitcast.115), calls=%async_computation | async-start | bytes 17039360 | tf_op jit(solution)/shard_map/all_to_all | solution.py:69
  114.2 2.9 collective-permute-start
  205.9 100.4 %all-to-all-start.2 = ((bf16[1,8,513,1024]{3,2,0,1:T(8,128)(2,1)}), bf16[1,8,513,1024]{3,2,0,1:T(8,128)(2,1)}, u32[]{:S(2)}, u32[]{:S(2)}) async-start(bf16[1,8,513,1024]{3,2,0,1:T(8,128)(2,1)} %bitcast.116), calls=%async_computation.2 | async-start | bytes 17039360 | tf_op jit(solution)/shard_map/all_to_all | solution.py:75
  214.6 21.6 %copy-start.5 = (bf16[1,1,1024,1536]{3,2,1,0:T(8,128)(2,1)S(1)}, bf16[1,1,1024,1536]{3,2,1,0:T(8,128)(2,1)}, u32[]{:S(2)}) copy-start(bf16[1,1,1024,1536]{3,2,1,0:T(8,128)(2,1)} %param.14) | copy-start | bytes 9437188
  390.1 100.9 %all-to-all-start.3 = ((bf16[1,8,513,1024]{3,2,0,1:T(8,128)(2,1)}), bf16[1,8,513,1024]{3,2,0,1:T(8,128)(2,1)}, u32[]{:S(2)}, u32[]{:S(2)}) async-start(bf16[1,8,513,1024]{3,2,0,1:T(8,128)(2,1)} %fusion.1), calls=%async_computation.3 | async-start | bytes 17039360 | tf_op jit(solution)/shard_map/all_to_all | solution.py:77
  417.9 82.0 %copy-start.2 = (s32[2048]{0:T(1024)S(1)}, s32[2048]{0:T(1024)}, u32[]{:S(2)}) copy-start(s32[2048]{0:T(1024)} %copy-done.1) | copy-start | bytes 24580
  417.9 82.0 %copy-start.4 = (s32[2048]{0:T(1024)S(1)}, s32[2048]{0:T(1024)}, u32[]{:S(2)}) copy-start(s32[2048]{0:T(1024)} %copy-done.3) | copy-start | bytes 24580
  491.0 100.5 %all-to-all-start.1 = ((bf16[1,8,513,1024]{3,2,0,1:T(8,128)(2,1)}), bf16[1,8,513,1024]{3,2,0,1:T(8,128)(2,1)}, u32[]{:S(2)}, u32[]{:S(2)}) async-start(bf16[1,8,513,1024]{3,2,0,1:T(8,128)(2,1)} %convert_bitcast_fusion), calls=%async_computation.1 | async-start | bytes 17039360 | tf_op jit(solution)/shard_map/all_to_all | solution.py:71
  643.3 45.6 %collective-permute-start.3 = (bf16[1024,1024]{1,0:T(8,128)(2,1)}, bf16[1024,1024]{1,0:T(8,128)(2,1)}, u32[]{:S(2)}, u32[]{:S(2)}) collective-permute-start(bf16[1024,1024]{1,0:T(8,128)(2,1)} %reduce_sum.35), channel_id=1, source_target_pairs={{8,0},{0,8},{9,1},{1,9},{10,2},{2,10},{11,3},{3,11},{12,4},{4,12},... | collective-permute-start | bytes 6291464 | tf_op jit(solution)/shard_map/ppermute | solution.py:79
where the time goes:
time: 706 us; the launch traced here: 692 us
  waiting for transfers between devices  233 us (33%)
  matrix products  205 us (29%)
  local copies, waits for them, and re-layouts  140 us (20%)
  other arithmetic  75.2 us (11%)
  starting transfers between devices  38 us (5%)
    all_to_all x1, waiting for transfers between devices, device_fn(): lax.all_to_all(dx_rows, 'expert', 1, 1, tiled=True).reshape(-1, model_dim)  73.1 us
    all_to_all x1, waiting for transfers between devices, device_fn(): do_rows = lax.all_to_all(do_send, 'expert', 1, 1, tiled=True)  49.5 us
    ppermute x1, waiting for transfers between devices, device_fn(): ids_mine = lax.ppermute(expert_ids[0], 'stage', send_next)  45.6 us
    dot_general x1, matrix products, expert_backward(): jnp.einsum('epcd,efd->epcf', do_rows, wd_loc, preferred_element_type=jnp....  40.4 us
    all_to_all x1, waiting for transfers between devices, device_fn(): x_rows = lax.all_to_all(x_send, 'expert', 1, 1, tiled=True)  36.4 us
    gather x2, local copies, waits for them, and re-layouts, gather_choices(): picked = jnp.take(rows_flat, slots.reshape(-1), axis=0)  31.1 us
    all_to_all x1, waiting for transfers between devices, device_fn(): lax.all_to_all(out_rows, 'expert', 1, 1, tiled=True).reshape(-1, model_dim)  26.6 us
    dot_general x1, matrix products, expert_backward(): jnp.einsum('epcf,edf->epcd', g_up, wu_loc, preferred_element_type=jnp.flo...  23.8 us
  transfers between devices with their start and end apart: 8, of which 6 were waited for; matrix products, arithmetic and copies ran while one was open for 35% of the time, Pallas kernels for 0%

commit v1 on v0

v1 whole, which is shorter than its diff:
```python
import functools

import jax
import jax.numpy as jnp
from jax import lax
from jax.experimental import pallas as pl
from jax.experimental.pallas import tpu as pltpu
from jax.sharding import PartitionSpec as P

MESH = pl.DeviceIdType.MESH
BF16 = jnp.bfloat16
F32 = jnp.float32
NN = (((1,), (0,)), ((), ()))
NT = (((1,), (1,)), ((), ()))
TN = (((0,), (0,)), ((), ()))
DEVS = 8
TILE = 512


def mm(lhs, rhs, dims=NN):
    return lax.dot_general(lhs, rhs, dims, preferred_element_type=F32)


def flip(a, b):
    out = 0
    for w in (1, 2, 4):
        p = (a // w) % 2
        q = (b // w) % 2
        out = out + w * (p + q - 2 * p * q)
    return out


def nth_offset(k):
    third, fourth = k // 3, k // 4
    return k + (third - fourth) * (1 - k // 6) - (fourth - k // 5)


def col(start, size):
    return pl.ds(pl.multiple_of(start, size), size)


def moe_kernel(rows, sent, tab_ref, x_ref, dy_ref, wg_hbm, wu_hbm, wd_hbm,
               y_ref, dx_ref, gwg_ref, gwu_ref, gwd_ref, xg, dyg, out_stage, dx_stage, out_back, dx_back,
               tabs, pos_s, gate_s, pos_y, gate_y, pos_x, wg, wu, wd, accg, accu, accd, xst, dyst, onehot, grow,
               xr, dor, hid, da, du, obuf, dbuf,
               load_sem, tab_send, tab_recv, z_send, x_send, dy_send, x_recv, dy_recv,
               out_send, out_recv, dxs_send, dxs_recv, loc_sem):
    tok, dim = x_ref.shape
    ffn = wg_hbm.shape[1]
    half = tok // 2
    st, me = lax.axis_index('stage'), lax.axis_index('expert')
    other = 1 - st
    part = [pl.ds(0, half), pl.ds(half, half)]

    barrier = pltpu.get_barrier_semaphore()
    for d in range(DEVS):
        if d:
            pl.semaphore_signal(barrier, inc=1, device_id=(st, flip(me, d)), device_id_type=MESH)
        pl.semaphore_signal(barrier, inc=1, device_id=(other, flip(me, d)), device_id_type=MESH)
    pl.semaphore_wait(barrier, 2 * DEVS - 1)

    def remote(src, dst, ssem, rsem, stage, dev):
        return pltpu.make_async_remote_copy(src_ref=src, dst_ref=dst, send_sem=ssem, recv_sem=rsem,
                                            device_id=(stage, dev), device_id_type=MESH)

    def push(src, dst, ssem, rsem, stage, dev):
        remote(src, dst, ssem, rsem, stage, dev).start()

    def tab_copy(d):
        return remote(tab_ref, tabs.at[d], tab_send.at[d], tab_recv.at[d], other, flip(me, d))

    for d in range(DEVS):
        tab_copy(d).start()
    loads = [pltpu.make_async_copy(src, dst, load_sem.at[n])
             for n, (src, dst) in enumerate(((wg_hbm, wg), (wu_hbm, wu), (wd_hbm, wd)))]
    for c in range(2):
        push(x_ref.at[part[c]], xg.at[0, part[c]], z_send.at[c], x_recv.at[0, c], other, me)
    for c in range(2):
        for n, b in enumerate((2, 4, 1)):
            push(dy_ref.at[part[c]], dyg.at[b, part[c]], dy_send.at[2 * n + c], dy_recv.at[b, c], st, flip(me, b))
    for cp in loads:
        cp.start()

    def got(buf, sems, d, c):
        remote(buf.at[d, part[c]], buf.at[d, part[c]], z_send.at[0], sems.at[d, c], st, me).wait_recv()

    @pl.loop(0, tok // 128)
    def _(n):
        accg[col(n * 128, 128), :] = jnp.zeros((128, ffn), F32)
        accu[col(n * 128, 128), :] = jnp.zeros((128, ffn), F32)

    @pl.loop(0, ffn // 128)
    def _(n):
        accd[col(n * 128, 128), :] = jnp.zeros((128, dim), F32)

    xst[...] = jnp.where(lax.broadcasted_iota(jnp.int32, (tok, tok), 0) < lax.broadcasted_iota(jnp.int32, (tok, tok), 1),
                         1.0, 0.0).astype(BF16)
    for d in range(DEVS):
        tab_copy(d).wait_recv()

    def plan(id0, id1, g0, g1, wanted):
        first, second = id0 == wanted, id1 == wanted
        named = jnp.logical_or(first, second)
        before = mm(jnp.where(named, 1.0, 0.0).astype(BF16), xst[...])
        return jnp.where(named, before, -1.0), jnp.where(first, g0, jnp.where(second, g1, 0.0))

    sub = lax.broadcasted_iota(jnp.int32, (DEVS, tok), 0)
    mine = jnp.zeros((DEVS, tok), F32) + me.astype(F32)
    each = jnp.bitwise_xor(sub, me).astype(F32)
    seen = tabs[...]
    pos, gate = plan(seen[:, 0, :], seen[:, 1, :], seen[:, 2, :], seen[:, 3, :], mine)
    for d in range(DEVS):
        pos_s[d] = pos[d:d + 1].astype(jnp.int32)
        gate_s[d] = gate[d:d + 1]
    here = tabs[0]
    pos, gate = plan(here[0:1], here[1:2], here[2:3], here[3:4], each)
    pos_y[...] = pos.T
    gate_y[...] = gate.T
    own = tab_ref[...]
    pos, _ = plan(own[0:1], own[1:2], own[2:3], own[3:4], each)
    pos_x[...] = pos.T

    for c in range(2):
        got(xg, x_recv, 0, c)
        for n, b in enumerate((2, 4, 1)):
            push(xg.at[0, part[c]], xg.at[b, part[c]], x_send.at[2 * n + c], x_recv.at[b, c], st, flip(me, b))

    def pass_on(buf, ssem, rsem):
        for d, to, c_on, n in ((2, 4, 1, 6), (4, 2, 0, 7)):
            for c in range(2):
                got(buf, rsem, d, c)
            push(buf.at[d, part[c_on]], buf.at[6, part[c_on]], ssem.at[n], rsem.at[6, c_on], st, flip(me, to))
        for m, d in enumerate((2, 4)):
            for c in range(2):
                push(buf.at[d, part[c]], buf.at[d + 1, part[c]], ssem.at[8 + 2 * m + c], rsem.at[d + 1, c], st, flip(me, 1))

    def pass_last(buf, ssem, rsem):
        for c in range(2):
            got(buf, rsem, 6, c)
            push(buf.at[6, part[c]], buf.at[7, part[c]], ssem.at[12 + c], rsem.at[7, c], st, flip(me, 1))

    pass_on(dyg, dy_send, dy_recv)
    for cp in loads:
        cp.wait()

    def out_copy(d):
        return remote(out_stage.at[d], out_back.at[d], out_send.at[d], out_recv.at[d], st, flip(me, d))

    def dx_copy(d):
        return remote(dx_stage.at[d], dx_back.at[d], dxs_send.at[d], dxs_recv.at[d], other, flip(me, d))

    def local(src, dst, n):
        return pltpu.make_async_copy(src, dst, loc_sem.at[n])

    third = rows // 3

    @pl.loop(0, DEVS)
    def _(k):
        d = nth_offset(k)

        @pl.when(k == 2)
        def _():
            pass_on(xg, x_send, x_recv)

        @pl.when(k == 4)
        def _():
            pass_last(dyg, dy_send, dy_recv)

        @pl.when(k == 5)
        def _():
            pass_last(xg, x_send, x_recv)

        @pl.when(d % 2 == 1)
        def _():
            for c in range(2):
                got(xg, x_recv, d, c)
                got(dyg, dy_recv, d, c)

        local(xg.at[d], xst, 0).start()

        @pl.when(k == 0)
        def _():
            local(dy_ref, dyst, 1).start()

        @pl.when(k > 0)
        def _():
            local(dyg.at[d], dyst, 1).start()

        @pl.loop(0, 3)
        def _(n):
            place = lax.broadcasted_iota(jnp.int32, (third, tok), 0) + n * third
            hit = place == pos_s[d]
            span = col(n * third, third)
            onehot[span, :] = jnp.where(hit, 1.0, 0.0).astype(BF16)
            grow[span, :] = jnp.sum(jnp.where(hit, gate_s[d], 0.0), axis=1, keepdims=True)

        local(xg.at[d], xst, 0).wait()
        local(dyg.at[d], dyst, 1).wait()

        @pl.loop(0, dim // TILE)
        def _(n):
            span = col(n * TILE, TILE)
            xr[:, span] = mm(onehot[...], xst[:, span]).astype(BF16)
            dor[:, span] = (grow[...] * mm(onehot[...], dyst[:, span])).astype(BF16)

        @pl.loop(0, ffn // TILE)
        def _(n):
            span = col(n * TILE, TILE)
            a = mm(xr[...], wg[:, span])
            u = mm(xr[...], wu[:, span])
            gh = mm(dor[...], wd[span, :], NT)
            sig = jax.nn.sigmoid(a)
            act = a * sig
            hid[:, span] = (act * u).astype(BF16)
            du[:, span] = (gh * act).astype(BF16)
            da[:, span] = (gh * u * sig * (1.0 + a * (1.0 - sig))).astype(BF16)

        @pl.loop(0, dim // TILE)
        def _(n):
            span = col(n * TILE, TILE)
            obuf[:, span] = mm(hid[...], wd[:, span]).astype(BF16)

        @pl.when(k == 0)
        def _():
            local(obuf, out_back.at[0], 0).start()

        @pl.when(k > 0)
        def _():
            local(obuf, out_stage.at[d], 0).start()

        @pl.loop(0, dim // TILE)
        def _(n):
            span = col(n * TILE, TILE)
            dbuf[:, span] = (mm(da[...], wg[span, :], NT) + mm(du[...], wu[span, :], NT)).astype(BF16)

        local(dbuf, dx_stage.at[d], 1).start()
        local(obuf, out_stage.at[d], 0).wait()

        @pl.when(k > 0)
        def _():
            out_copy(d).start()

        local(dbuf, dx_stage.at[d], 1).wait()
        dx_copy(d).start()

        @pl.loop(0, dim // TILE)
        def _(m):
            over = col(m * TILE, TILE)

            @pl.loop(0, ffn // TILE)
            def _(n):
                span = col(n * TILE, TILE)
                accg[over, span] += mm(xr[:, over], da[:, span], TN)
                accu[over, span] += mm(xr[:, over], du[:, span], TN)
                accd[span, over] += mm(hid[:, span], dor[:, over], TN)

    for acc, buf in ((accg, wg), (accu, wu), (accd, wd)):
        @pl.loop(0, acc.shape[0] // 128)
        def _(n, acc=acc, buf=buf):
            span = col(n * 128, 128)
            buf[span, :] = acc[span, :].astype(BF16)
    stores = [pltpu.make_async_copy(src, dst, load_sem.at[n])
              for n, (src, dst) in enumerate(((wg, gwg_ref), (wu, gwu_ref), (wd, gwd_ref)))]
    for cp in stores:
        cp.start()

    @pl.loop(0, tok // 128)
    def _(n):
        accg[col(n * 128, 128), :] = jnp.zeros((128, ffn), F32)
        accu[col(n * 128, 128), :] = jnp.zeros((128, ffn), F32)

    @pl.loop(0, DEVS)
    def _(k):
        d = nth_offset(k)

        @pl.when(k > 0)
        def _():
            out_copy(d).wait_recv()

        dx_copy(d).wait_recv()
        local(out_back.at[d], obuf, 0).start()
        local(dx_back.at[d], dbuf, 1).start()
        local(out_back.at[d], obuf, 0).wait()
        local(dx_back.at[d], dbuf, 1).wait()

        @pl.loop(0, tok // 256)
        def _(n):
            over = col(n * 256, 256)
            place = lax.broadcasted_iota(jnp.int32, (256, rows), 1)
            lane = lax.broadcasted_iota(jnp.int32, (256, DEVS), 1) == d

            def pick(ref):
                return jnp.sum(jnp.where(lane, ref[over, :], 0.0), axis=1, keepdims=True)

            sel = jnp.where(place == pick(pos_y).astype(jnp.int32), 1.0, 0.0).astype(BF16)
            accg[over, 0:dim] += pick(gate_y) * mm(sel, obuf[...])
            sel = jnp.where(place == pick(pos_x).astype(jnp.int32), 1.0, 0.0).astype(BF16)
            accu[over, 0:dim] += mm(sel, dbuf[...])

    @pl.loop(0, tok // 128)
    def _(n):
        span = col(n * 128, 128)
        xst[span, :] = accg[span, 0:dim].astype(BF16)
        dyst[span, :] = accu[span, 0:dim].astype(BF16)

    ends = [local(xst, y_ref, 0), local(dyst, dx_ref, 1)]
    for cp in ends:
        cp.start()
    for cp in ends + stores:
        cp.wait()
    for sems, count in ((z_send, 2), (x_send, 14), (dy_send, 14)):
        for n in range(count):
            remote(xg.at[0, part[0]], xg.at[0, part[0]], sems.at[n], sems.at[n], st, me).wait_send()
    for d in range(DEVS):
        tab_copy(d).wait_send()
        dx_copy(d).wait_send()
        if d:
            out_copy(d).wait_send()


def moe_call(tab, x, dy, wg, wu, wd, cap):
    tok, dim = x.shape
    ffn = wg.shape[1]
    rows = -(-cap // 48) * 48
    sent = -(-cap // 8) * 8
    any_spec = pl.BlockSpec(memory_space=pl.ANY)
    vmem = pl.BlockSpec(memory_space=pltpu.VMEM)
    shape = jax.ShapeDtypeStruct
    out_shape = [shape((tok, dim), BF16)] * 2 + [shape(wg.shape, BF16), shape(wu.shape, BF16), shape(wd.shape, BF16)]
    out_shape += [shape((DEVS, tok, dim), BF16)] * 2 + [shape((DEVS, rows, dim), BF16)] * 4
    dma, vm = pltpu.SemaphoreType.DMA, pltpu.VMEM
    scratch = [
        vm((DEVS, 8, tok), F32), vm((DEVS, 1, tok), jnp.int32), vm((DEVS, 1, tok), F32),
        vm((tok, DEVS), F32), vm((tok, DEVS), F32), vm((tok, DEVS), F32),
        vm((dim, ffn), BF16), vm((dim, ffn), BF16), vm((ffn, dim), BF16),
        vm((dim, ffn), F32), vm((dim, ffn), F32), vm((ffn, dim), F32),
        vm((tok, dim), BF16), vm((tok, dim), BF16), vm((rows, tok), BF16), vm((rows, 1), F32),
        vm((rows, dim), BF16), vm((rows, dim), BF16), vm((rows, ffn), BF16), vm((rows, ffn), BF16), vm((rows, ffn), BF16),
        vm((rows, dim), BF16), vm((rows, dim), BF16),
        dma((3,)), dma((DEVS,)), dma((DEVS,)), dma((2,)), dma((14,)), dma((14,)), dma((DEVS, 2)), dma((DEVS, 2)),
        dma((DEVS,)), dma((DEVS,)), dma((DEVS,)), dma((DEVS,)), dma((2,)),
    ]
    return pl.pallas_call(
        functools.partial(moe_kernel, rows, sent),
        out_shape=out_shape,
        in_specs=[vmem] + [any_spec] * 5,
        out_specs=[any_spec] * len(out_shape),
        scratch_shapes=scratch,
        compiler_params=pltpu.CompilerParams(collective_id=0, has_side_effects=True, vmem_limit_bytes=67043328),
    )(tab, x, dy, wg, wu, wd)


def solution(mesh):
    stages, ep_size = mesh.shape['stage'], mesh.shape['expert']
    assert stages == 2 and ep_size == DEVS
    tok_spec = P('stage', 'expert', None)
    w_spec = P('stage', 'expert', None, None)

    def device_fn(x_acts, expert_ids, gate_vals, w_gate, w_up, w_down, grad_out):
        tok, top_k = expert_ids.shape[1:]
        cap = 2 * tok * top_k // (w_gate.shape[1] * ep_size) + 1
        tab = jnp.concatenate([expert_ids[0].T.astype(F32), gate_vals[0].T, jnp.zeros((4, tok), F32)], axis=0)
        outs = moe_call(tab, x_acts[0], grad_out[0], w_gate[0, 0], w_up[0, 0], w_down[0, 0], cap)
        y, dx, gwg, gwu, gwd = outs[:5]
        return y[None], dx[None], gwg[None, None], gwu[None, None], gwd[None, None]

    return jax.shard_map(device_fn, mesh=mesh, in_specs=(tok_spec, tok_spec, tok_spec, w_spec, w_spec, w_spec, tok_spec), out_specs=(tok_spec, tok_spec, w_spec, w_spec, w_spec), check_vma=False)
```

time: 706 us -> 399 us (0.57); the launches traced: 692 us -> 398 us
  Pallas kernels: 0 us -> 383 us
  waiting for transfers between devices: 233 us -> 0 us
  matrix products: 205 us -> 0 us
  local copies, waits for them, and re-layouts: 140 us -> 12.4 us
  other arithmetic: 75.2 us -> 2.08 us
  starting transfers between devices: 38 us -> 0 us
    pallas_call x0 -> x1, Pallas kernels: none -> 383 us  [moe_call(): pl.pallas_call(functools.partial(moe_kernel, rows, sent), out_shape=out_s...]
    dot_general x9 -> x0, matrix products: 205 us -> none  [the longest x1 40.4 us: expert_backward(): jnp.einsum('epcd,efd->epcf', do_rows, wd_loc, preferred_element_type=jnp....]
    all_to_all x4 -> x0, waiting for transfers between devices: 186 us -> none  [the longest x1 73.1 us: device_fn(): lax.all_to_all(dx_rows, 'expert', 1, 1, tiled=True).reshape(-1, model_dim)]
    gather x4 -> x0, local copies, waits for them, and re-layouts: 73.7 us -> none  [the longest x2 31.1 us: gather_choices(): picked = jnp.take(rows_flat, slots.reshape(-1), axis=0)]
    ppermute x4 -> x0, waiting for transfers between devices: 47 us -> none  [the longest x1 45.6 us: device_fn(): ids_mine = lax.ppermute(expert_ids[0], 'stage', send_next)]
    reshape x6 -> x0, local copies, waits for them, and re-layouts: 45.1 us -> none  [the longest x1 9.14 us: device_fn(): lax.all_to_all(out_rows, 'expert', 1, 1, tiled=True).reshape(-1, model_dim)]
    all_to_all x4 -> x0, starting transfers between devices: 32.9 us -> none  [the longest x1 9.19 us: device_fn(): lax.all_to_all(dx_rows, 'expert', 1, 1, tiled=True).reshape(-1, model_dim)]
    reduce_sum x3 -> x0, other arithmetic: 26.2 us -> none  [the longest x1 13.5 us: device_fn(): jnp.sum(gate_mine[:, :, None] * picked.astype(jnp.float32), axis=1)]
  transfers between devices with their start and end apart: 8 -> 0, of which waited for: 6 -> 0; matrix products, arithmetic and copies ran while one was open for 35% -> 0% of each run, Pallas kernels for 0% -> 0%
where the time goes in v1:
time: 399 us; the launch traced here: 398 us
  Pallas kernels  383 us (96%)
  local copies, waits for them, and re-layouts  12.4 us (3%)
    pallas_call x1, Pallas kernels, moe_call(): pl.pallas_call(functools.partial(moe_kernel, rows, sent), out_shape=out_s...  383 us
    unnamed x13, local copies, waits for them, and re-layouts  12.3 us

profile of v1, /device:TPU:1, one launch (start us, length us, event | category | flops | bytes accessed | tf_op | source)
XLA Modules:
  0.0 398.2 jit_solution(14761501661340383210)
XLA Ops:
  0.6 0.1 pad.2.clone
  0.7 0.7 convert_bitcast_fusion
  1.4 1.4 maximum_maximum_fusion.tab_ref
  2.8 383.1 %shard_map.110 = (bf16[1024,1024]{1,0:T(8,128)(2,1)}, bf16[1024,1024]{1,0:T(8,128)(2,1)}, bf16[1024,1536]{1,0:T(8,128)(2,1)}, bf16[1024,1536]{1,0:T(8,128)(2,1)}...) custom-call(f32[8,1024]{1,0:T(8,128)} %maximum_maximum_fusion.tab_re, ...), custom_call_target="tpu_custom_call" | custom-call | tf_op jit(solution)/shard_map/pallas_call | solution.py:343
  385.9 0.0 copy-start.3
  385.9 0.0 copy-start.2
  385.9 3.2 copy.17
  389.1 0.0 copy-done.3
  389.1 1.3 copy.18
  390.5 0.0 copy-done.2
  390.5 0.0 copy-start.1
  390.5 1.7 copy.19
  392.1 1.4 copy-done.1
  393.5 0.0 copy-start
  393.5 1.7 copy.20
  395.1 1.4 copy-done
  396.5 1.7 copy.21
  (1 shorter events, 0.0 us)
Async XLA Ops:
  385.9 3.3 copy-start.3
  385.9 4.6 %copy-start.2 = (bf16[1024,1536]{1,0:T(8,128)(2,1)S(1)}, bf16[1024,1536]{1,0:T(8,128)(2,1)}, u32[]{:S(2)}) copy-start(bf16[1024,1536]{1,0:T(8,128)(2,1)} %get-tuple-element.12) | copy-start | bytes 9437188
  390.5 3.0 copy-start.1
  393.5 3.0 copy-start

commit v2 on v1

--- a/solution.py
+++ b/solution.py
@@ -105,10 +105,10 @@
         return jnp.where(named, before, -1.0), jnp.where(first, g0, jnp.where(second, g1, 0.0))
 
     sub = lax.broadcasted_iota(jnp.int32, (DEVS, tok), 0)
-    mine = jnp.zeros((DEVS, tok), F32) + me.astype(F32)
+    always = jnp.zeros((DEVS, tok), F32) + me.astype(F32)
     each = jnp.bitwise_xor(sub, me).astype(F32)
     seen = tabs[...]
-    pos, gate = plan(seen[:, 0, :], seen[:, 1, :], seen[:, 2, :], seen[:, 3, :], mine)
+    pos, gate = plan(seen[:, 0, :], seen[:, 1, :], seen[:, 2, :], seen[:, 3, :], always)
     for d in range(DEVS):
         pos_s[d] = pos[d:d + 1].astype(jnp.int32)
         gate_s[d] = gate[d:d + 1]
@@ -157,6 +157,7 @@
     @pl.loop(0, DEVS)
     def _(k):
         d = nth_offset(k)
+        mine = col((k % 2) * rows, rows)
 
         @pl.when(k == 2)
         def _():
@@ -200,25 +201,25 @@
         @pl.loop(0, dim // TILE)
         def _(n):
             span = col(n * TILE, TILE)
-            xr[:, span] = mm(onehot[...], xst[:, span]).astype(BF16)
-            dor[:, span] = (grow[...] * mm(onehot[...], dyst[:, span])).astype(BF16)
+            xr[mine, span] = mm(onehot[...], xst[:, span]).astype(BF16)
+            dor[mine, span] = (grow[...] * mm(onehot[...], dyst[:, span])).astype(BF16)
 
         @pl.loop(0, ffn // TILE)
         def _(n):
             span = col(n * TILE, TILE)
-            a = mm(xr[...], wg[:, span])
-            u = mm(xr[...], wu[:, span])
-            gh = mm(dor[...], wd[span, :], NT)
+            a = mm(xr[mine, :], wg[:, span])
+            u = mm(xr[mine, :], wu[:, span])
+            gh = mm(dor[mine, :], wd[span, :], NT)
             sig = jax.nn.sigmoid(a)
             act = a * sig
-            hid[:, span] = (act * u).astype(BF16)
-            du[:, span] = (gh * act).astype(BF16)
-            da[:, span] = (gh * u * sig * (1.0 + a * (1.0 - sig))).astype(BF16)
+            hid[mine, span] = (act * u).astype(BF16)
+            du[mine, span] = (gh * act).astype(BF16)
+            da[mine, span] = (gh * u * sig * (1.0 + a * (1.0 - sig))).astype(BF16)
 
         @pl.loop(0, dim // TILE)
         def _(n):
             span = col(n * TILE, TILE)
-            obuf[:, span] = mm(hid[...], wd[:, span]).astype(BF16)
+            obuf[:, span] = mm(hid[mine, :], wd[:, span]).astype(BF16)
 
         @pl.when(k == 0)
         def _():
@@ -231,28 +232,40 @@
         @pl.loop(0, dim // TILE)
         def _(n):
             span = col(n * TILE, TILE)
-            dbuf[:, span] = (mm(da[...], wg[span, :], NT) + mm(du[...], wu[span, :], NT)).astype(BF16)
+            dbuf[:, span] = (mm(da[mine, :], wg[span, :], NT) + mm(du[mine, :], wu[span, :], NT)).astype(BF16)
 
         local(dbuf, dx_stage.at[d], 1).start()
         local(obuf, out_stage.at[d], 0).wait()
-
-        @pl.when(k > 0)
+        paired = (k // 2 == 1) | (k // 2 == 2)
+        later = k % 2 == 1
+
+        @pl.when((k > 0) & jnp.logical_not(paired & later))
         def _():
             out_copy(d).start()
 
         local(dbuf, dx_stage.at[d], 1).wait()
-        dx_copy(d).start()
-
-        @pl.loop(0, dim // TILE)
-        def _(m):
-            over = col(m * TILE, TILE)
-
-            @pl.loop(0, ffn // TILE)
-            def _(n):
-                span = col(n * TILE, TILE)
-                accg[over, span] += mm(xr[:, over], da[:, span], TN)
-                accu[over, span] += mm(xr[:, over], du[:, span], TN)
-                accd[span, over] += mm(hid[:, span], dor[:, over], TN)
+
+        @pl.when(jnp.logical_not(paired & jnp.logical_not(later)))
+        def _():
+            dx_copy(d).start()
+
+        @pl.when(paired & later)
+        def _():
+            out_copy(d).start()
+            dx_copy(nth_offset(k - 1)).start()
+
+        @pl.when(later)
+        def _():
+            @pl.loop(0, dim // TILE)
+            def _(m):
+                over = col(m * TILE, TILE)
+
+                @pl.loop(0, ffn // TILE)
+                def _(n):
+                    span = col(n * TILE, TILE)
+                    accg[over, span] += mm(xr[:, over], da[:, span], TN)
+                    accu[over, span] += mm(xr[:, over], du[:, span], TN)
+                    accd[span, over] += mm(hid[:, span], dor[:, over], TN)
 
     for acc, buf in ((accg, wg), (accu, wu), (accd, wd)):
         @pl.loop(0, acc.shape[0] // 128)
@@ -335,7 +348,7 @@
         vm((dim, ffn), BF16), vm((dim, ffn), BF16), vm((ffn, dim), BF16),
         vm((dim, ffn), F32), vm((dim, ffn), F32), vm((ffn, dim), F32),
         vm((tok, dim), BF16), vm((tok, dim), BF16), vm((rows, tok), BF16), vm((rows, 1), F32),
-        vm((rows, dim), BF16), vm((rows, dim), BF16), vm((rows, ffn), BF16), vm((rows, ffn), BF16), vm((rows, ffn), BF16),
+        vm((2 * rows, dim), BF16), vm((2 * rows, dim), BF16), vm((2 * rows, ffn), BF16), vm((2 * rows, ffn), BF16), vm((2 * rows, ffn), BF16),
         vm((rows, dim), BF16), vm((rows, dim), BF16),
         dma((3,)), dma((DEVS,)), dma((DEVS,)), dma((2,)), dma((14,)), dma((14,)), dma((DEVS, 2)), dma((DEVS, 2)),
         dma((DEVS,)), dma((DEVS,)), dma((DEVS,)), dma((DEVS,)), dma((2,)),

time: 399 us -> 369 us (0.925)
  Pallas kernels: 383 us -> 353 us
    pallas_call x1, Pallas kernels: 383 us -> 353 us  [moe_call(): pl.pallas_call(functools.partial(moe_kernel, rows, sent), out_shape=out_s...]
where the time goes in v2:
time: 369 us; the launch traced here: 368 us
  Pallas kernels  353 us (96%)
  local copies, waits for them, and re-layouts  12.4 us (3%)
    pallas_call x1, Pallas kernels, moe_call(): pl.pallas_call(functools.partial(moe_kernel, rows, sent), out_shape=out_s...  353 us
    unnamed x13, local copies, waits for them, and re-layouts  12.3 us

profile of v2, /device:TPU:1, one launch (start us, length us, event | category | flops | bytes accessed | tf_op | source)
XLA Modules:
  0.0 368.2 jit_solution(7586961347784365428)
XLA Ops:
  0.6 0.1 pad.2.clone
  0.7 0.7 convert_bitcast_fusion
  1.4 1.4 maximum_maximum_fusion.tab_ref
  2.8 353.1 %shard_map.110 = (bf16[1024,1024]{1,0:T(8,128)(2,1)}, bf16[1024,1024]{1,0:T(8,128)(2,1)}, bf16[1024,1536]{1,0:T(8,128)(2,1)}, bf16[1024,1536]{1,0:T(8,128)(2,1)}...) custom-call(f32[8,1024]{1,0:T(8,128)} %maximum_maximum_fusion.tab_re, ...), custom_call_target="tpu_custom_call" | custom-call | tf_op jit(solution)/shard_map/pallas_call | solution.py:356
  355.9 0.0 copy-start.3
  355.9 0.0 copy-start.2
  355.9 3.2 copy.17
  359.2 0.0 copy-done.3
  359.2 1.3 copy.18
  360.5 0.0 copy-done.2
  360.5 0.0 copy-start.1
  360.5 1.7 copy.19
  362.2 1.4 copy-done.1
  363.5 0.0 copy-start
  363.5 1.7 copy.20
  365.2 1.4 copy-done
  366.6 1.7 copy.21
  (1 shorter events, 0.0 us)
Async XLA Ops:
  355.9 3.3 copy-start.3
  355.9 4.6 %copy-start.2 = (bf16[1024,1536]{1,0:T(8,128)(2,1)S(1)}, bf16[1024,1536]{1,0:T(8,128)(2,1)}, u32[]{:S(2)}) copy-start(bf16[1024,1536]{1,0:T(8,128)(2,1)} %get-tuple-element.12) | copy-start | bytes 9437188
  360.5 3.0 copy-start.1
  363.5 3.0 copy-start

commit v3 on v2

--- a/solution.py
+++ b/solution.py
@@ -39,12 +39,26 @@
     return pl.ds(pl.multiple_of(start, size), size)
 
 
-def moe_kernel(rows, sent, tab_ref, x_ref, dy_ref, wg_hbm, wu_hbm, wd_hbm,
-               y_ref, dx_ref, gwg_ref, gwu_ref, gwd_ref, xg, dyg, out_stage, dx_stage, out_back, dx_back,
-               tabs, pos_s, gate_s, pos_y, gate_y, pos_x, wg, wu, wd, accg, accu, accd, xst, dyst, onehot, grow,
-               xr, dor, hid, da, du, obuf, dbuf,
+def select(mask):
+    return jnp.where(mask, 1.0, 0.0).astype(BF16)
+
+
+def greet(st, me):
+    barrier = pltpu.get_barrier_semaphore()
+    for d in range(DEVS):
+        if d:
+            pl.semaphore_signal(barrier, inc=1, device_id=(st, flip(me, d)), device_id_type=MESH)
+        pl.semaphore_signal(barrier, inc=1, device_id=(1 - st, flip(me, d)), device_id_type=MESH)
+    pl.semaphore_wait(barrier, 2 * DEVS - 1)
+
+
+def moe_kernel(rows, base, tab_ref, x_ref, dy_ref, wg_hbm, wu_hbm, wd_hbm,
+               y_ref, dx_ref, gwg_ref, gwu_ref, gwd_ref, out_stage, dx_stage, pos_y_ref, gate_y_ref, pos_x_ref, flag_ref,
+               xg, dyg, out_back, dx_back, over_own, over_peer, over_sum, over_back,
+               tabs, pos_s, gate_s, shift_s, pos_y, gate_y, pos_x, over_y, over_x, flag_own, flag_peer, wg, wu, wd, accg, accu, accd, xst, dyst, onehot, grow,
+               xr, dor, hid, da, du, obuf, dbuf, ovv, ovw, move,
                load_sem, tab_send, tab_recv, z_send, x_send, dy_send, x_recv, dy_recv,
-               out_send, out_recv, dxs_send, dxs_recv, loc_sem):
+               out_send, out_recv, dxs_send, dxs_recv, pair_send, pair_recv, sum_send, sum_recv, flag_sem, loc_sem):
     tok, dim = x_ref.shape
     ffn = wg_hbm.shape[1]
     half = tok // 2
@@ -52,12 +66,8 @@
     other = 1 - st
     part = [pl.ds(0, half), pl.ds(half, half)]
 
-    barrier = pltpu.get_barrier_semaphore()
-    for d in range(DEVS):
-        if d:
-            pl.semaphore_signal(barrier, inc=1, device_id=(st, flip(me, d)), device_id_type=MESH)
-        pl.semaphore_signal(barrier, inc=1, device_id=(other, flip(me, d)), device_id_type=MESH)
-    pl.semaphore_wait(barrier, 2 * DEVS - 1)
+    extra = rows - base
+    greet(st, me)
 
     def remote(src, dst, ssem, rsem, stage, dev):
         return pltpu.make_async_remote_copy(src_ref=src, dst_ref=dst, send_sem=ssem, recv_sem=rsem,
@@ -98,27 +108,48 @@
     for d in range(DEVS):
         tab_copy(d).wait_recv()
 
-    def plan(id0, id1, g0, g1, wanted):
-        first, second = id0 == wanted, id1 == wanted
+    sub = lax.broadcasted_iota(jnp.int32, (DEVS, tok), 0)
+    each = sub.astype(F32)
+    sub_col = lax.broadcasted_iota(jnp.int32, (DEVS, 1), 0)
+
+    def earlier(named):
+        return jnp.where(named, mm(select(named), xst[...]), -1.0)
+
+    def spilled(named):
+        past = jnp.maximum(jnp.sum(jnp.where(named, 1.0, 0.0), axis=1, keepdims=True) - base, 0.0)
+        start, total = jnp.zeros((DEVS, 1), F32), jnp.zeros((1, 1), F32)
+        for e in range(DEVS):
+            start = jnp.where(sub_col == e, total, start)
+            total = total + past[e:e + 1]
+        return start, total
+
+    def source_tables(tab):
+        first, second = tab[0:1] == each, tab[1:2] == each
         named = jnp.logical_or(first, second)
-        before = mm(jnp.where(named, 1.0, 0.0).astype(BF16), xst[...])
-        return jnp.where(named, before, -1.0), jnp.where(first, g0, jnp.where(second, g1, 0.0))
-
-    sub = lax.broadcasted_iota(jnp.int32, (DEVS, tok), 0)
-    always = jnp.zeros((DEVS, tok), F32) + me.astype(F32)
-    each = jnp.bitwise_xor(sub, me).astype(F32)
+        pos = earlier(named)
+        gate = jnp.where(first, tab[2:3], jnp.where(second, tab[3:4], 0.0))
+        start, _ = spilled(named)
+        shared = jnp.where(pos >= base, pos - base + start + 1.0, 0.0)
+        place = [jnp.sum(jnp.where(which, shared, 0.0), axis=0, keepdims=True) - 1.0 for which in (first, second)]
+        over = jnp.where(sub == 0, place[0], jnp.where(sub == 1, place[1], jnp.where(sub == 2, tab[2:3], tab[3:4])))
+        return pos.T, gate.T, over.T
+
     seen = tabs[...]
-    pos, gate = plan(seen[:, 0, :], seen[:, 1, :], seen[:, 2, :], seen[:, 3, :], always)
+    me_f = me.astype(F32)
+    first, second = seen[:, 0, :] == me_f, seen[:, 1, :] == me_f
+    pos = earlier(jnp.logical_or(first, second))
+    gate = jnp.where(first, seen[:, 2, :], jnp.where(second, seen[:, 3, :], 0.0))
+    most = jnp.zeros((1, 1), F32)
     for d in range(DEVS):
         pos_s[d] = pos[d:d + 1].astype(jnp.int32)
         gate_s[d] = gate[d:d + 1]
-    here = tabs[0]
-    pos, gate = plan(here[0:1], here[1:2], here[2:3], here[3:4], each)
-    pos_y[...] = pos.T
-    gate_y[...] = gate.T
-    own = tab_ref[...]
-    pos, _ = plan(own[0:1], own[1:2], own[2:3], own[3:4], each)
-    pos_x[...] = pos.T
+        start, total = spilled(jnp.logical_or(seen[d, 0:1] == each, seen[d, 1:2] == each))
+        mine = jnp.sum(jnp.where(sub_col == me, start, 0.0), axis=0, keepdims=True)
+        shift_s[d] = jnp.broadcast_to(mine, (1, 128)).astype(jnp.int32)
+        most = jnp.maximum(most, total)
+    flag_own[...] = jnp.broadcast_to(jnp.where(most > extra, 1.0, 0.0), (8, 128))
+    pos_y[...], gate_y[...], over_y[...] = source_tables(tabs[0])
+    pos_x[...], _, over_x[...] = source_tables(tab_ref[...])
 
     for c in range(2):
         got(xg, x_recv, 0, c)
@@ -144,13 +175,35 @@
         cp.wait()
 
     def out_copy(d):
-        return remote(out_stage.at[d], out_back.at[d], out_send.at[d], out_recv.at[d], st, flip(me, d))
+        return remote(out_stage.at[d, pl.ds(0, base)], out_back.at[d], out_send.at[d], out_recv.at[d], st, flip(me, d))
 
     def dx_copy(d):
-        return remote(dx_stage.at[d], dx_back.at[d], dxs_send.at[d], dxs_recv.at[d], other, flip(me, d))
+        return remote(dx_stage.at[d, pl.ds(0, base)], dx_back.at[d], dxs_send.at[d], dxs_recv.at[d], other, flip(me, d))
 
     def local(src, dst, n):
         return pltpu.make_async_copy(src, dst, loc_sem.at[n])
+
+    def pair_copy(t, d):
+        return remote(over_own.at[t, d], over_peer.at[t, d // 2], pair_send.at[t, d // 2], pair_recv.at[t, d // 2], st, flip(me, 1))
+
+    def sum_copy(t, j):
+        return remote(over_sum.at[t, j], over_back.at[t, j], sum_send.at[t, j], sum_recv.at[t, j], other if t else st, flip(me, 2 * j))
+
+    def merge(j):
+        for t in range(2):
+            pair_copy(t, 2 * j).wait_recv()
+            local(over_own.at[t, 2 * j], ovv.at[t], t).start()
+            local(over_peer.at[t, j], ovw.at[t], 2 + t).start()
+        for t in range(2):
+            local(over_own.at[t, 2 * j], ovv.at[t], t).wait()
+            local(over_peer.at[t, j], ovw.at[t], 2 + t).wait()
+            ovv[t] = (ovv[t].astype(F32) + ovw[t].astype(F32)).astype(BF16)
+            to = over_back if t == 0 and j == 0 else over_sum
+            local(ovv.at[t], to.at[t, j], t).start()
+        for t in range(2):
+            local(ovv.at[t], over_sum.at[t, j], t).wait()
+            if t or j:
+                sum_copy(t, j).start()
 
     third = rows // 3
 
@@ -195,6 +248,8 @@
             onehot[span, :] = jnp.where(hit, 1.0, 0.0).astype(BF16)
             grow[span, :] = jnp.sum(jnp.where(hit, gate_s[d], 0.0), axis=1, keepdims=True)
 
+        move[...] = select(lax.broadcasted_iota(jnp.int32, (extra, extra), 0)
+                           == lax.broadcasted_iota(jnp.int32, (extra, extra), 1) + shift_s[d][:, 0:1])
         local(xg.at[d], xst, 0).wait()
         local(dyg.at[d], dyst, 1).wait()
 
@@ -221,13 +276,9 @@
             span = col(n * TILE, TILE)
             obuf[:, span] = mm(hid[mine, :], wd[:, span]).astype(BF16)
 
-        @pl.when(k == 0)
-        def _():
-            local(obuf, out_back.at[0], 0).start()
-
-        @pl.when(k > 0)
-        def _():
-            local(obuf, out_stage.at[d], 0).start()
+        local(obuf, out_stage.at[d], 0).start()
+        ovv[0] = mm(move[...], obuf[base:, :]).astype(BF16)
+        local(ovv.at[0], over_own.at[0, d], 2).start()
 
         @pl.loop(0, dim // TILE)
         def _(n):
@@ -235,7 +286,17 @@
             dbuf[:, span] = (mm(da[mine, :], wg[span, :], NT) + mm(du[mine, :], wu[span, :], NT)).astype(BF16)
 
         local(dbuf, dx_stage.at[d], 1).start()
+        ovv[1] = mm(move[...], dbuf[base:, :]).astype(BF16)
+        local(ovv.at[1], over_own.at[1, d], 3).start()
         local(obuf, out_stage.at[d], 0).wait()
+        for t in range(2):
+            local(ovv.at[t], over_own.at[t, d], 2 + t).wait()
+
+        @pl.when(d % 2 == 1)
+        def _():
+            for t in range(2):
+                pair_copy(t, d).start()
+
         paired = (k // 2 == 1) | (k // 2 == 2)
         later = k % 2 == 1
 
@@ -253,6 +314,10 @@
         def _():
             out_copy(d).start()
             dx_copy(nth_offset(k - 1)).start()
+
+        @pl.when(k == DEVS - 1)
+        def _():
+            merge(3)
 
         @pl.when(later)
         def _():
@@ -266,6 +331,18 @@
                     accg[over, span] += mm(xr[:, over], da[:, span], TN)
                     accu[over, span] += mm(xr[:, over], du[:, span], TN)
                     accd[span, over] += mm(hid[:, span], dor[:, over], TN)
+
+        @pl.when(k == 3)
+        def _():
+            merge(0)
+
+        @pl.when(k == 5)
+        def _():
+            merge(1)
+            merge(2)
+
+    flag_copy = remote(flag_own, flag_peer, flag_sem.at[0], flag_sem.at[1], other, me)
+    flag_copy.start()
 
     for acc, buf in ((accg, wg), (accu, wu), (accd, wd)):
         @pl.loop(0, acc.shape[0] // 128)
@@ -286,29 +363,54 @@
     def _(k):
         d = nth_offset(k)
 
+        @pl.when(k == 0)
+        def _():
+            local(out_stage.at[0, pl.ds(0, base)], obuf.at[pl.ds(0, base)], 0).start()
+
         @pl.when(k > 0)
         def _():
             out_copy(d).wait_recv()
+            local(out_back.at[d], obuf.at[pl.ds(0, base)], 0).start()
 
         dx_copy(d).wait_recv()
-        local(out_back.at[d], obuf, 0).start()
-        local(dx_back.at[d], dbuf, 1).start()
-        local(out_back.at[d], obuf, 0).wait()
-        local(dx_back.at[d], dbuf, 1).wait()
+        local(dx_back.at[d], dbuf.at[pl.ds(0, base)], 1).start()
+        local(out_back.at[d], obuf.at[pl.ds(0, base)], 0).wait()
+        local(dx_back.at[d], dbuf.at[pl.ds(0, base)], 1).wait()
 
         @pl.loop(0, tok // 256)
         def _(n):
             over = col(n * 256, 256)
-            place = lax.broadcasted_iota(jnp.int32, (256, rows), 1)
-            lane = lax.broadcasted_iota(jnp.int32, (256, DEVS), 1) == d
+            place = lax.broadcasted_iota(jnp.int32, (256, base), 1)
+            lane = lax.broadcasted_iota(jnp.int32, (256, DEVS), 1) == flip(me, d)
 
             def pick(ref):
                 return jnp.sum(jnp.where(lane, ref[over, :], 0.0), axis=1, keepdims=True)
 
-            sel = jnp.where(place == pick(pos_y).astype(jnp.int32), 1.0, 0.0).astype(BF16)
-            accg[over, 0:dim] += pick(gate_y) * mm(sel, obuf[...])
-            sel = jnp.where(place == pick(pos_x).astype(jnp.int32), 1.0, 0.0).astype(BF16)
-            accu[over, 0:dim] += mm(sel, dbuf[...])
+            accg[over, 0:dim] += pick(gate_y) * mm(select(place == pick(pos_y).astype(jnp.int32)), obuf[0:base, :])
+            accu[over, 0:dim] += mm(select(place == pick(pos_x).astype(jnp.int32)), dbuf[0:base, :])
+
+    for j in range(4):
+        for t in range(2):
+            if t or j:
+                sum_copy(t, j).wait_recv()
+            local(over_back.at[t, j], ovw.at[t] if j else ovv.at[t], t).start()
+        for t in range(2):
+            local(over_back.at[t, j], ovw.at[t] if j else ovv.at[t], t).wait()
+            if j:
+                ovv[t] = (ovv[t].astype(F32) + ovw[t].astype(F32)).astype(BF16)
+
+    @pl.loop(0, tok // 256)
+    def _(n):
+        over = col(n * 256, 256)
+        place = lax.broadcasted_iota(jnp.int32, (256, extra), 1)
+        at_y, at_x = over_y[over, :], over_x[over, :]
+
+        def chosen(tab, c):
+            return place == tab[:, c:c + 1].astype(jnp.int32)
+
+        for c in range(2):
+            accg[over, 0:dim] += at_y[:, 2 + c:3 + c] * mm(select(chosen(at_y, c)), ovv[0])
+        accu[over, 0:dim] += mm(select(jnp.logical_or(chosen(at_x, 0), chosen(at_x, 1))), ovv[1])
 
     @pl.loop(0, tok // 128)
     def _(n):
@@ -316,7 +418,10 @@
         xst[span, :] = accg[span, 0:dim].astype(BF16)
         dyst[span, :] = accu[span, 0:dim].astype(BF16)
 
-    ends = [local(xst, y_ref, 0), local(dyst, dx_ref, 1)]
+    flag_copy.wait()
+    flag_own[...] = jnp.maximum(flag_own[...], flag_peer[...])
+    ends = [local(xst, y_ref, 0), local(dyst, dx_ref, 1), local(flag_own, flag_ref, 2), local(pos_y, pos_y_ref, 3),
+            local(gate_y, gate_y_ref, 4), local(pos_x, pos_x_ref, 5)]
     for cp in ends:
         cp.start()
     for cp in ends + stores:
@@ -329,32 +434,125 @@
         dx_copy(d).wait_send()
         if d:
             out_copy(d).wait_send()
-
-
-def moe_call(tab, x, dy, wg, wu, wd, cap):
+    for j in range(4):
+        for t in range(2):
+            pair_copy(t, 2 * j).wait_send()
+            if t or j:
+                sum_copy(t, j).wait_send()
+
+
+def return_kernel(out_stage, dx_stage, pos_y, gate_y, pos_x, y_ref, dx_ref, out_back, dx_back,
+                  acc_y, acc_x, obuf, dbuf, ybuf, xbuf, out_send, out_recv, dxs_send, dxs_recv, loc_sem):
+    tok, dim = y_ref.shape
+    rows = out_stage.shape[1]
+    st, me = lax.axis_index('stage'), lax.axis_index('expert')
+    greet(st, me)
+
+    def out_copy(d):
+        return pltpu.make_async_remote_copy(src_ref=out_stage.at[d], dst_ref=out_back.at[d], send_sem=out_send.at[d],
+                                            recv_sem=out_recv.at[d], device_id=(st, flip(me, d)), device_id_type=MESH)
+
+    def dx_copy(d):
+        return pltpu.make_async_remote_copy(src_ref=dx_stage.at[d], dst_ref=dx_back.at[d], send_sem=dxs_send.at[d],
+                                            recv_sem=dxs_recv.at[d], device_id=(1 - st, flip(me, d)), device_id_type=MESH)
+
+    def local(src, dst, n):
+        return pltpu.make_async_copy(src, dst, loc_sem.at[n])
+
+    for d in range(DEVS):
+        dx_copy(d).start()
+        if d:
+            out_copy(d).start()
+    acc_y[...] = jnp.zeros_like(acc_y)
+    acc_x[...] = jnp.zeros_like(acc_x)
+
+    @pl.loop(0, DEVS)
+    def _(d):
+        @pl.when(d == 0)
+        def _():
+            local(out_stage.at[0], obuf, 0).start()
+
+        @pl.when(d > 0)
+        def _():
+            out_copy(d).wait_recv()
+            local(out_back.at[d], obuf, 0).start()
+
+        dx_copy(d).wait_recv()
+        local(dx_back.at[d], dbuf, 1).start()
+        local(out_back.at[d], obuf, 0).wait()
+        local(dx_back.at[d], dbuf, 1).wait()
+
+        @pl.loop(0, tok // 256)
+        def _(n):
+            over = col(n * 256, 256)
+            place = lax.broadcasted_iota(jnp.int32, (256, rows), 1)
+            lane = lax.broadcasted_iota(jnp.int32, (256, DEVS), 1) == flip(me, d)
+
+            def pick(ref):
+                return jnp.sum(jnp.where(lane, ref[over, :], 0.0), axis=1, keepdims=True)
+
+            acc_y[over, :] += pick(gate_y) * mm(select(place == pick(pos_y).astype(jnp.int32)), obuf[...])
+            acc_x[over, :] += mm(select(place == pick(pos_x).astype(jnp.int32)), dbuf[...])
+
+    ybuf[...] = acc_y[...].astype(BF16)
+    xbuf[...] = acc_x[...].astype(BF16)
+    ends = [local(ybuf, y_ref, 0), local(xbuf, dx_ref, 1)]
+    for cp in ends:
+        cp.start()
+    for cp in ends:
+        cp.wait()
+    for d in range(DEVS):
+        dx_copy(d).wait_send()
+        if d:
+            out_copy(d).wait_send()
+
+
+def return_call(out_stage, dx_stage, pos_y, gate_y, pos_x):
+    rows, dim = out_stage.shape[1:]
+    tok = pos_y.shape[0]
+    any_spec = pl.BlockSpec(memory_space=pl.ANY)
+    vmem = pl.BlockSpec(memory_space=pltpu.VMEM)
+    dma, vm, shape = pltpu.SemaphoreType.DMA, pltpu.VMEM, jax.ShapeDtypeStruct
+    outs = pl.pallas_call(
+        return_kernel,
+        out_shape=[shape((tok, dim), BF16)] * 2 + [shape(out_stage.shape, BF16)] * 2,
+        in_specs=[any_spec] * 2 + [vmem] * 3,
+        out_specs=[any_spec] * 4,
+        scratch_shapes=[vm((tok, dim), F32)] * 2 + [vm((rows, dim), BF16)] * 2 + [vm((tok, dim), BF16)] * 2
+        + [dma((DEVS,))] * 4 + [dma((2,))],
+        compiler_params=pltpu.CompilerParams(collective_id=1, has_side_effects=True),
+    )(out_stage, dx_stage, pos_y, gate_y, pos_x)
+    return outs[0], outs[1]
+
+
+def moe_call(tab, x, dy, wg, wu, wd, cap, mean):
     tok, dim = x.shape
     ffn = wg.shape[1]
     rows = -(-cap // 48) * 48
-    sent = -(-cap // 8) * 8
+    base = mean // 32 * 28
+    extra = rows - base
     any_spec = pl.BlockSpec(memory_space=pl.ANY)
     vmem = pl.BlockSpec(memory_space=pltpu.VMEM)
     shape = jax.ShapeDtypeStruct
     out_shape = [shape((tok, dim), BF16)] * 2 + [shape(wg.shape, BF16), shape(wu.shape, BF16), shape(wd.shape, BF16)]
-    out_shape += [shape((DEVS, tok, dim), BF16)] * 2 + [shape((DEVS, rows, dim), BF16)] * 4
+    out_shape += [shape((DEVS, rows, dim), BF16)] * 2 + [shape((tok, DEVS), F32)] * 3 + [shape((8, 128), F32)]
+    out_shape += [shape((DEVS, tok, dim), BF16)] * 2 + [shape((DEVS, base, dim), BF16)] * 2
+    out_shape += [shape((2, DEVS, extra, dim), BF16)] + [shape((2, 4, extra, dim), BF16)] * 3
     dma, vm = pltpu.SemaphoreType.DMA, pltpu.VMEM
     scratch = [
-        vm((DEVS, 8, tok), F32), vm((DEVS, 1, tok), jnp.int32), vm((DEVS, 1, tok), F32),
-        vm((tok, DEVS), F32), vm((tok, DEVS), F32), vm((tok, DEVS), F32),
+        vm((DEVS, 8, tok), F32), vm((DEVS, 1, tok), jnp.int32), vm((DEVS, 1, tok), F32), vm((DEVS, 1, 128), jnp.int32),
+        vm((tok, DEVS), F32), vm((tok, DEVS), F32), vm((tok, DEVS), F32), vm((tok, DEVS), F32), vm((tok, DEVS), F32),
+        vm((8, 128), F32), vm((8, 128), F32),
         vm((dim, ffn), BF16), vm((dim, ffn), BF16), vm((ffn, dim), BF16),
         vm((dim, ffn), F32), vm((dim, ffn), F32), vm((ffn, dim), F32),
         vm((tok, dim), BF16), vm((tok, dim), BF16), vm((rows, tok), BF16), vm((rows, 1), F32),
         vm((2 * rows, dim), BF16), vm((2 * rows, dim), BF16), vm((2 * rows, ffn), BF16), vm((2 * rows, ffn), BF16), vm((2 * rows, ffn), BF16),
-        vm((rows, dim), BF16), vm((rows, dim), BF16),
+        vm((rows, dim), BF16), vm((rows, dim), BF16), vm((2, extra, dim), BF16), vm((2, extra, dim), BF16), vm((extra, extra), BF16),
         dma((3,)), dma((DEVS,)), dma((DEVS,)), dma((2,)), dma((14,)), dma((14,)), dma((DEVS, 2)), dma((DEVS, 2)),
-        dma((DEVS,)), dma((DEVS,)), dma((DEVS,)), dma((DEVS,)), dma((2,)),
+        dma((DEVS,)), dma((DEVS,)), dma((DEVS,)), dma((DEVS,)), dma((2, 4)), dma((2, 4)), dma((2, 4)), dma((2, 4)), dma((2,)), dma((6,)),
     ]
     return pl.pallas_call(
-        functools.partial(moe_kernel, rows, sent),
+        functools.partial(moe_kernel, rows, base),
         out_shape=out_shape,
         in_specs=[vmem] + [any_spec] * 5,
         out_specs=[any_spec] * len(out_shape),
@@ -373,8 +571,9 @@
         tok, top_k = expert_ids.shape[1:]
         cap = 2 * tok * top_k // (w_gate.shape[1] * ep_size) + 1
         tab = jnp.concatenate([expert_ids[0].T.astype(F32), gate_vals[0].T, jnp.zeros((4, tok), F32)], axis=0)
-        outs = moe_call(tab, x_acts[0], grad_out[0], w_gate[0, 0], w_up[0, 0], w_down[0, 0], cap)
+        outs = moe_call(tab, x_acts[0], grad_out[0], w_gate[0, 0], w_up[0, 0], w_down[0, 0], cap, tok * top_k // ep_size)
         y, dx, gwg, gwu, gwd = outs[:5]
+        y, dx = lax.cond(outs[10][0, 0] > 0, return_call, lambda *_: (y, dx), *outs[5:10])
         return y[None], dx[None], gwg[None, None], gwu[None, None], gwd[None, None]
 
     return jax.shard_map(device_fn, mesh=mesh, in_specs=(tok_spec, tok_spec, tok_spec, w_spec, w_spec, w_spec, tok_spec), out_specs=(tok_spec, tok_spec, w_spec, w_spec, w_spec), check_vma=False)

time: 369 us -> 354 us (0.959)
  Pallas kernels: 353 us -> 334 us
    pallas_call x1, Pallas kernels: 353 us -> 334 us  [moe_call(): pl.pallas_call(functools.partial(moe_kernel, rows, base), out_shape=out_s...]
where the time goes in v3:
time: 354 us; the launch traced here: 352 us
  Pallas kernels  334 us (94%)
  local copies, waits for them, and re-layouts  14.9 us (4%)
    pallas_call x1, Pallas kernels, moe_call(): pl.pallas_call(functools.partial(moe_kernel, rows, base), out_shape=out_s...  334 us
    unnamed x13, local copies, waits for them, and re-layouts  13.6 us

profile of v3, /device:TPU:1, one launch (start us, length us, event | category | flops | bytes accessed | tf_op | source)
XLA Modules:
  0.0 351.8 jit_solution(6719865267680669116)
XLA Ops:
  0.6 0.1 pad.2.clone
  0.7 0.7 convert_bitcast_fusion
  1.4 1.4 maximum_maximum_fusion.tab_ref
  2.8 333.5 %shard_map.110 = (bf16[1024,1024]{1,0:T(8,128)(2,1)}, bf16[1024,1024]{1,0:T(8,128)(2,1)}, bf16[1024,1536]{1,0:T(8,128)(2,1)}, bf16[1024,1536]{1,0:T(8,128)(2,1)}...) custom-call(f32[8,1024]{1,0:T(8,128)} %maximum_maximum_fusion.tab_re, ...), custom_call_target="tpu_custom_call" | custom-call | tf_op jit(solution)/shard_map/pallas_call | solution.py:554
  336.3 1.2 slice.3
  338.2 0.0 copy-start.3
  338.2 3.2 copy.21
  341.4 0.0 copy-done.3
  341.4 0.0 copy-start.2
  341.4 1.3 copy.22
  342.7 1.3 copy-done.2
  344.1 0.0 copy-start.1
  344.1 1.7 copy.23
  345.7 1.4 copy-done.1
  347.1 0.0 copy-start
  347.1 1.7 copy.24
  348.8 1.4 copy-done
  350.1 1.7 copy.25
  (2 shorter events, 0.0 us)
Async XLA Ops:
  338.2 3.2 copy-start.3
  341.4 2.6 copy-start.2
  344.1 3.0 copy-start.1
  347.1 3.0 copy-start

commit v4 on v3

--- a/solution.py
+++ b/solution.py
@@ -55,15 +55,17 @@
 def moe_kernel(rows, base, tab_ref, x_ref, dy_ref, wg_hbm, wu_hbm, wd_hbm,
                y_ref, dx_ref, gwg_ref, gwu_ref, gwd_ref, out_stage, dx_stage, pos_y_ref, gate_y_ref, pos_x_ref, flag_ref,
                xg, dyg, out_back, dx_back, over_own, over_peer, over_sum, over_back,
+               keep_x, keep_do, keep_h, keep_da, keep_du,
                tabs, pos_s, gate_s, shift_s, pos_y, gate_y, pos_x, over_y, over_x, flag_own, flag_peer, wg, wu, wd, accg, accu, accd, xst, dyst, onehot, grow,
-               xr, dor, hid, da, du, obuf, dbuf, ovv, ovw, move,
+               xr, dor, hid, da, du, obuf, dbuf, ovv, ova, ovw, move,
                load_sem, tab_send, tab_recv, z_send, x_send, dy_send, x_recv, dy_recv,
-               out_send, out_recv, dxs_send, dxs_recv, pair_send, pair_recv, sum_send, sum_recv, flag_sem, loc_sem):
+               out_send, out_recv, dxs_send, dxs_recv, pair_send, pair_recv, sum_send, sum_recv, flag_sem, loc_sem, keep_sem):
     tok, dim = x_ref.shape
     ffn = wg_hbm.shape[1]
     half = tok // 2
     st, me = lax.axis_index('stage'), lax.axis_index('expert')
     other = 1 - st
+    core = me % 2
     part = [pl.ds(0, half), pl.ds(half, half)]
 
     extra = rows - base
@@ -83,11 +85,21 @@
         tab_copy(d).start()
     loads = [pltpu.make_async_copy(src, dst, load_sem.at[n])
              for n, (src, dst) in enumerate(((wg_hbm, wg), (wu_hbm, wu), (wd_hbm, wd)))]
-    for c in range(2):
-        push(x_ref.at[part[c]], xg.at[0, part[c]], z_send.at[c], x_recv.at[0, c], other, me)
-    for c in range(2):
-        for n, b in enumerate((2, 4, 1)):
-            push(dy_ref.at[part[c]], dyg.at[b, part[c]], dy_send.at[2 * n + c], dy_recv.at[b, c], st, flip(me, b))
+    def send_x():
+        for c in range(2):
+            push(x_ref.at[part[c]], xg.at[0, part[c]], z_send.at[c], x_recv.at[0, c], other, me)
+
+    def send_dy(targets):
+        for n, b in targets:
+            for c in range(2):
+                push(dy_ref.at[part[c]], dyg.at[b, part[c]], dy_send.at[2 * n + c], dy_recv.at[b, c], st, flip(me, b))
+
+    @pl.when(core == 0)
+    def _():
+        send_x()
+        send_dy(((0, 2), (1, 4)))
+
+    send_dy(((2, 1),))
     for cp in loads:
         cp.start()
 
@@ -151,10 +163,11 @@
     pos_y[...], gate_y[...], over_y[...] = source_tables(tabs[0])
     pos_x[...], _, over_x[...] = source_tables(tab_ref[...])
 
-    for c in range(2):
-        got(xg, x_recv, 0, c)
-        for n, b in enumerate((2, 4, 1)):
-            push(xg.at[0, part[c]], xg.at[b, part[c]], x_send.at[2 * n + c], x_recv.at[b, c], st, flip(me, b))
+    def spread_x():
+        for c in range(2):
+            got(xg, x_recv, 0, c)
+            for n, b in enumerate((2, 4, 1)):
+                push(xg.at[0, part[c]], xg.at[b, part[c]], x_send.at[2 * n + c], x_recv.at[b, c], st, flip(me, b))
 
     def pass_on(buf, ssem, rsem):
         for d, to, c_on, n in ((2, 4, 1, 6), (4, 2, 0, 7)):
@@ -170,10 +183,48 @@
             got(buf, rsem, 6, c)
             push(buf.at[6, part[c]], buf.at[7, part[c]], ssem.at[12 + c], rsem.at[7, c], st, flip(me, 1))
 
-    pass_on(dyg, dy_send, dy_recv)
+    def order(k):
+        near = nth_offset(k)
+        return near + core * (1 - 2 * (near % 2))
+
+    def fetch(k):
+        d = order(k)
+
+        @pl.when((d % 2 == 1) & (k > 0))
+        def _():
+            for c in range(2):
+                got(xg, x_recv, d, c)
+
+        @pl.when(d % 2 == 1)
+        def _():
+            for c in range(2):
+                got(dyg, dy_recv, d, c)
+
+        pltpu.make_async_copy(xg.at[d], xst, loc_sem.at[4]).start()
+
+        @pl.when(d == 0)
+        def _():
+            pltpu.make_async_copy(dy_ref, dyst, loc_sem.at[5]).start()
+
+        @pl.when(d > 0)
+        def _():
+            pltpu.make_async_copy(dyg.at[d], dyst, loc_sem.at[5]).start()
+
     for cp in loads:
         cp.wait()
 
+    @pl.when(core == 0)
+    def _():
+        spread_x()
+        pass_on(dyg, dy_send, dy_recv)
+
+    @pl.when(core == 1)
+    def _():
+        for c in range(2):
+            got(xg, x_recv, 1, c)
+        send_x()
+        send_dy(((0, 2), (1, 4)))
+
     def out_copy(d):
         return remote(out_stage.at[d, pl.ds(0, base)], out_back.at[d], out_send.at[d], out_recv.at[d], st, flip(me, d))
 
@@ -189,30 +240,104 @@
     def sum_copy(t, j):
         return remote(over_sum.at[t, j], over_back.at[t, j], sum_send.at[t, j], sum_recv.at[t, j], other if t else st, flip(me, 2 * j))
 
-    def merge(j):
+    def merge_load(j):
         for t in range(2):
             pair_copy(t, 2 * j).wait_recv()
-            local(over_own.at[t, 2 * j], ovv.at[t], t).start()
-            local(over_peer.at[t, j], ovw.at[t], 2 + t).start()
+            local(over_own.at[t, 2 * j], ova.at[t], 6 + t).start()
+            local(over_peer.at[t, j], ovw.at[t], 8 + t).start()
+
+    def merge_add(j):
         for t in range(2):
-            local(over_own.at[t, 2 * j], ovv.at[t], t).wait()
-            local(over_peer.at[t, j], ovw.at[t], 2 + t).wait()
-            ovv[t] = (ovv[t].astype(F32) + ovw[t].astype(F32)).astype(BF16)
+            local(over_own.at[t, 2 * j], ova.at[t], 6 + t).wait()
+            local(over_peer.at[t, j], ovw.at[t], 8 + t).wait()
+            ova[t] = (ova[t].astype(F32) + ovw[t].astype(F32)).astype(BF16)
             to = over_back if t == 0 and j == 0 else over_sum
-            local(ovv.at[t], to.at[t, j], t).start()
+            local(ova.at[t], to.at[t, j], 6 + t).start()
+
+    def merge_send(j):
         for t in range(2):
-            local(ovv.at[t], over_sum.at[t, j], t).wait()
+            local(ova.at[t], over_sum.at[t, j], 6 + t).wait()
             if t or j:
                 sum_copy(t, j).start()
 
+    def merges(k, step):
+        for j, (low, high) in enumerate(((2, 3), (3, 5), (4, 6), (7, 8))):
+            @pl.when(k == low + core * (high - low))
+            def _(j=j):
+                step(j)
+
+    kept = ((xr, keep_x), (dor, keep_do), (hid, keep_h), (da, keep_da), (du, keep_du))
+
+    def region(k):
+        return col((k % 2) * rows, rows)
+
+    def keep(k):
+        return [pltpu.make_async_copy(buf.at[region(k)], hbm.at[k - 3], keep_sem.at[5 * (k % 2) + n])
+                for n, (buf, hbm) in enumerate(kept)]
+
+    def bring(k):
+        return [pltpu.make_async_copy(hbm.at[k - 3], buf.at[region(k + 1)], keep_sem.at[5 * ((k + 1) % 2) + n])
+                for n, (buf, hbm) in enumerate(kept)]
+
+    def weight_grads(span_k, middle):
+        @pl.loop(0, dim // TILE)
+        def _(m):
+            over = col(m * TILE, TILE)
+
+            @pl.when(m == 1)
+            def _():
+                middle()
+
+            @pl.loop(0, ffn // TILE)
+            def _(n):
+                span = col(n * TILE, TILE)
+                accg[over, span] += mm(xr[span_k, over], da[span_k, span], TN)
+                accu[over, span] += mm(xr[span_k, over], du[span_k, span], TN)
+                accd[span, over] += mm(hid[span_k, span], dor[span_k, over], TN)
+
+    def send_back(k):
+        d = order(k)
+        local(obuf, out_stage.at[d], 0).wait()
+        local(dbuf, dx_stage.at[d], 1).wait()
+        for t in range(2):
+            local(ovv.at[t], over_own.at[t, d], 2 + t).wait()
+        paired = (k // 2 == 1) | (k // 2 == 2)
+        later = k % 2 == 1
+
+        @pl.when((d > 0) & jnp.logical_not(paired & later))
+        def _():
+            out_copy(d).start()
+
+        @pl.when(jnp.logical_not(paired & jnp.logical_not(later)))
+        def _():
+            dx_copy(d).start()
+
+        @pl.when(paired & later)
+        def _():
+            out_copy(d).start()
+            dx_copy(order(k - 1)).start()
+
+        @pl.when(d % 2 == 1)
+        def _():
+            for t in range(2):
+                pair_copy(t, d).start()
+
     third = rows // 3
 
     @pl.loop(0, DEVS)
     def _(k):
-        d = nth_offset(k)
-        mine = col((k % 2) * rows, rows)
-
-        @pl.when(k == 2)
+        d = order(k)
+        mine = region(k)
+
+        @pl.when((k == 1) & (core == 1))
+        def _():
+            spread_x()
+
+        @pl.when((k == 2) & (core == 1))
+        def _():
+            pass_on(dyg, dy_send, dy_recv)
+
+        @pl.when(k == 2 + core)
         def _():
             pass_on(xg, x_send, x_recv)
 
@@ -220,25 +345,13 @@
         def _():
             pass_last(dyg, dy_send, dy_recv)
 
-        @pl.when(k == 5)
+        @pl.when((k == 5) & (core == 0))
         def _():
             pass_last(xg, x_send, x_recv)
 
-        @pl.when(d % 2 == 1)
-        def _():
-            for c in range(2):
-                got(xg, x_recv, d, c)
-                got(dyg, dy_recv, d, c)
-
-        local(xg.at[d], xst, 0).start()
-
-        @pl.when(k == 0)
-        def _():
-            local(dy_ref, dyst, 1).start()
-
-        @pl.when(k > 0)
-        def _():
-            local(dyg.at[d], dyst, 1).start()
+        @pl.when(k < 3)
+        def _():
+            fetch(k)
 
         @pl.loop(0, 3)
         def _(n):
@@ -250,14 +363,27 @@
 
         move[...] = select(lax.broadcasted_iota(jnp.int32, (extra, extra), 0)
                            == lax.broadcasted_iota(jnp.int32, (extra, extra), 1) + shift_s[d][:, 0:1])
-        local(xg.at[d], xst, 0).wait()
-        local(dyg.at[d], dyst, 1).wait()
+        @pl.when(k > 4)
+        def _():
+            for cp in keep(k - 2):
+                cp.wait()
+
+        local(xg.at[d], xst, 4).wait()
+        local(dyg.at[d], dyst, 5).wait()
 
         @pl.loop(0, dim // TILE)
         def _(n):
             span = col(n * TILE, TILE)
             xr[mine, span] = mm(onehot[...], xst[:, span]).astype(BF16)
             dor[mine, span] = (grow[...] * mm(onehot[...], dyst[:, span])).astype(BF16)
+
+        @pl.when((k == 2) | (k > 3))
+        def _():
+            send_back(k - 1)
+
+        @pl.when((k == 3) | (k == 4))
+        def _():
+            fetch(k + 1)
 
         @pl.loop(0, ffn // TILE)
         def _(n):
@@ -271,6 +397,13 @@
             du[mine, span] = (gh * act).astype(BF16)
             da[mine, span] = (gh * u * sig * (1.0 + a * (1.0 - sig))).astype(BF16)
 
+        @pl.when((k > 2) & (k < DEVS - 1))
+        def _():
+            for cp in keep(k):
+                cp.start()
+
+        merges(k, merge_load)
+
         @pl.loop(0, dim // TILE)
         def _(n):
             span = col(n * TILE, TILE)
@@ -280,6 +413,8 @@
         ovv[0] = mm(move[...], obuf[base:, :]).astype(BF16)
         local(ovv.at[0], over_own.at[0, d], 2).start()
 
+        merges(k, merge_add)
+
         @pl.loop(0, dim // TILE)
         def _(n):
             span = col(n * TILE, TILE)
@@ -288,58 +423,56 @@
         local(dbuf, dx_stage.at[d], 1).start()
         ovv[1] = mm(move[...], dbuf[base:, :]).astype(BF16)
         local(ovv.at[1], over_own.at[1, d], 3).start()
-        local(obuf, out_stage.at[d], 0).wait()
-        for t in range(2):
-            local(ovv.at[t], over_own.at[t, d], 2 + t).wait()
-
-        @pl.when(d % 2 == 1)
-        def _():
-            for t in range(2):
-                pair_copy(t, d).start()
-
-        paired = (k // 2 == 1) | (k // 2 == 2)
-        later = k % 2 == 1
-
-        @pl.when((k > 0) & jnp.logical_not(paired & later))
-        def _():
-            out_copy(d).start()
-
-        local(dbuf, dx_stage.at[d], 1).wait()
-
-        @pl.when(jnp.logical_not(paired & jnp.logical_not(later)))
-        def _():
-            dx_copy(d).start()
-
-        @pl.when(paired & later)
-        def _():
-            out_copy(d).start()
-            dx_copy(nth_offset(k - 1)).start()
-
-        @pl.when(k == DEVS - 1)
-        def _():
-            merge(3)
-
-        @pl.when(later)
-        def _():
-            @pl.loop(0, dim // TILE)
-            def _(m):
-                over = col(m * TILE, TILE)
-
-                @pl.loop(0, ffn // TILE)
-                def _(n):
-                    span = col(n * TILE, TILE)
-                    accg[over, span] += mm(xr[:, over], da[:, span], TN)
-                    accu[over, span] += mm(xr[:, over], du[:, span], TN)
-                    accd[span, over] += mm(hid[:, span], dor[:, over], TN)
-
-        @pl.when(k == 3)
-        def _():
-            merge(0)
-
-        @pl.when(k == 5)
-        def _():
-            merge(1)
-            merge(2)
+        merges(k, merge_send)
+
+        @pl.when((k == 5) & (core == 1))
+        def _():
+            pass_last(xg, x_send, x_recv)
+
+        @pl.when((k == 2) | (k == 5) | (k == 6))
+        def _():
+            fetch(k + 1)
+
+        @pl.when(k == 0)
+        def _():
+            send_back(k)
+            weight_grads(mine, lambda: None)
+
+        @pl.when(k == 2)
+        def _():
+            weight_grads(slice(None), lambda: send_back(k))
+
+    last = DEVS - 1
+    send_back(last)
+    for cp in keep(last - 1):
+        cp.wait()
+    for cp in bring(3):
+        cp.start()
+
+    @pl.when(core == 1)
+    def _():
+        merge_load(3)
+        merge_add(3)
+
+    def send_last():
+        @pl.when(core == 1)
+        def _():
+            merge_send(3)
+
+    weight_grads(region(last), send_last)
+    for cp in bring(4):
+        cp.start()
+    for k in (3, 4):
+        for cp in bring(k):
+            cp.wait()
+    weight_grads(slice(None), lambda: None)
+    for k in (5, 6):
+        for cp in bring(k):
+            cp.start()
+    for k in (5, 6):
+        for cp in bring(k):
+            cp.wait()
+    weight_grads(slice(None), lambda: None)
 
     flag_copy = remote(flag_own, flag_peer, flag_sem.at[0], flag_sem.at[1], other, me)
     flag_copy.start()
@@ -359,23 +492,35 @@
         accg[col(n * 128, 128), :] = jnp.zeros((128, ffn), F32)
         accu[col(n * 128, 128), :] = jnp.zeros((128, ffn), F32)
 
+    def back(k):
+        return pl.ds(pl.multiple_of((k % 2) * base, 16), base)
+
+    def load_back(k):
+        d = nth_offset(k)
+
+        @pl.when(k == 0)
+        def _():
+            local(out_stage.at[0, pl.ds(0, base)], obuf.at[back(k)], 0).start()
+
+        @pl.when(k > 0)
+        def _():
+            out_copy(d).wait_recv()
+            local(out_back.at[d], obuf.at[back(k)], k % 2).start()
+
+        dx_copy(d).wait_recv()
+        local(dx_back.at[d], dbuf.at[back(k)], 2 + k % 2).start()
+
+    load_back(0)
+
     @pl.loop(0, DEVS)
     def _(k):
         d = nth_offset(k)
-
-        @pl.when(k == 0)
-        def _():
-            local(out_stage.at[0, pl.ds(0, base)], obuf.at[pl.ds(0, base)], 0).start()
-
-        @pl.when(k > 0)
-        def _():
-            out_copy(d).wait_recv()
-            local(out_back.at[d], obuf.at[pl.ds(0, base)], 0).start()
-
-        dx_copy(d).wait_recv()
-        local(dx_back.at[d], dbuf.at[pl.ds(0, base)], 1).start()
-        local(out_back.at[d], obuf.at[pl.ds(0, base)], 0).wait()
-        local(dx_back.at[d], dbuf.at[pl.ds(0, base)], 1).wait()
+        local(out_back.at[d], obuf.at[back(k)], k % 2).wait()
+        local(dx_back.at[d], dbuf.at[back(k)], 2 + k % 2).wait()
+
+        @pl.when(k < DEVS - 1)
+        def _():
+            load_back(k + 1)
 
         @pl.loop(0, tok // 256)
         def _(n):
@@ -386,18 +531,20 @@
             def pick(ref):
                 return jnp.sum(jnp.where(lane, ref[over, :], 0.0), axis=1, keepdims=True)
 
-            accg[over, 0:dim] += pick(gate_y) * mm(select(place == pick(pos_y).astype(jnp.int32)), obuf[0:base, :])
-            accu[over, 0:dim] += mm(select(place == pick(pos_x).astype(jnp.int32)), dbuf[0:base, :])
-
+            accg[over, 0:dim] += pick(gate_y) * mm(select(place == pick(pos_y).astype(jnp.int32)), obuf[back(k), :])
+            accu[over, 0:dim] += mm(select(place == pick(pos_x).astype(jnp.int32)), dbuf[back(k), :])
+
+    held = [[xst.at[pl.ds(j * extra, extra)] if j < 3 else ovv.at[0] for j in range(4)],
+            [dyst.at[pl.ds(j * extra, extra)] if j < 3 else ovv.at[1] for j in range(4)]]
     for j in range(4):
         for t in range(2):
             if t or j:
                 sum_copy(t, j).wait_recv()
-            local(over_back.at[t, j], ovw.at[t] if j else ovv.at[t], t).start()
-        for t in range(2):
-            local(over_back.at[t, j], ovw.at[t] if j else ovv.at[t], t).wait()
-            if j:
-                ovv[t] = (ovv[t].astype(F32) + ovw[t].astype(F32)).astype(BF16)
+            local(over_back.at[t, j], held[t][j], 4 * t + j).start()
+    for t in range(2):
+        for j in range(4):
+            local(over_back.at[t, j], held[t][j], 4 * t + j).wait()
+        ovv[t] = sum(held[t][j][...].astype(F32) for j in range(4)).astype(BF16)
 
     @pl.loop(0, tok // 256)
     def _(n):
@@ -538,6 +685,7 @@
     out_shape += [shape((DEVS, rows, dim), BF16)] * 2 + [shape((tok, DEVS), F32)] * 3 + [shape((8, 128), F32)]
     out_shape += [shape((DEVS, tok, dim), BF16)] * 2 + [shape((DEVS, base, dim), BF16)] * 2
     out_shape += [shape((2, DEVS, extra, dim), BF16)] + [shape((2, 4, extra, dim), BF16)] * 3
+    out_shape += [shape((4, rows, dim), BF16)] * 2 + [shape((4, rows, ffn), BF16)] * 3
     dma, vm = pltpu.SemaphoreType.DMA, pltpu.VMEM
     scratch = [
         vm((DEVS, 8, tok), F32), vm((DEVS, 1, tok), jnp.int32), vm((DEVS, 1, tok), F32), vm((DEVS, 1, 128), jnp.int32),
@@ -547,9 +695,9 @@
         vm((dim, ffn), F32), vm((dim, ffn), F32), vm((ffn, dim), F32),
         vm((tok, dim), BF16), vm((tok, dim), BF16), vm((rows, tok), BF16), vm((rows, 1), F32),
         vm((2 * rows, dim), BF16), vm((2 * rows, dim), BF16), vm((2 * rows, ffn), BF16), vm((2 * rows, ffn), BF16), vm((2 * rows, ffn), BF16),
-        vm((rows, dim), BF16), vm((rows, dim), BF16), vm((2, extra, dim), BF16), vm((2, extra, dim), BF16), vm((extra, extra), BF16),
+        vm((rows, dim), BF16), vm((rows, dim), BF16), vm((2, extra, dim), BF16), vm((2, extra, dim), BF16), vm((2, extra, dim), BF16), vm((extra, extra), BF16),
         dma((3,)), dma((DEVS,)), dma((DEVS,)), dma((2,)), dma((14,)), dma((14,)), dma((DEVS, 2)), dma((DEVS, 2)),
-        dma((DEVS,)), dma((DEVS,)), dma((DEVS,)), dma((DEVS,)), dma((2, 4)), dma((2, 4)), dma((2, 4)), dma((2, 4)), dma((2,)), dma((6,)),
+        dma((DEVS,)), dma((DEVS,)), dma((DEVS,)), dma((DEVS,)), dma((2, 4)), dma((2, 4)), dma((2, 4)), dma((2, 4)), dma((2,)), dma((10,)), dma((10,)),
     ]
     return pl.pallas_call(
         functools.partial(moe_kernel, rows, base),

time: 354 us -> 317 us (0.90)
  Pallas kernels: 334 us -> 298 us
    pallas_call x1, Pallas kernels: 334 us -> 298 us  [moe_call(): pl.pallas_call(functools.partial(moe_kernel, rows, base), out_shape=out_s...]
where the time goes in v4:
time: 317 us; the launch traced here: 316 us
  Pallas kernels  298 us (94%)
  local copies, waits for them, and re-layouts  14.9 us (5%)
    pallas_call x1, Pallas kernels, moe_call(): pl.pallas_call(functools.partial(moe_kernel, rows, base), out_shape=out_s...  298 us
    unnamed x13, local copies, waits for them, and re-layouts  13.6 us

profile of v4, /device:TPU:1, one launch (start us, length us, event | category | flops | bytes accessed | tf_op | source)
XLA Modules:
  0.0 316.4 jit_solution(3122992982555442206)
XLA Ops:
  0.6 0.1 pad.2.clone
  0.7 0.7 convert_bitcast_fusion
  1.4 1.4 maximum_maximum_fusion.tab_ref
  2.8 298.1 %shard_map.110 = (bf16[1024,1024]{1,0:T(8,128)(2,1)}, bf16[1024,1024]{1,0:T(8,128)(2,1)}, bf16[1024,1536]{1,0:T(8,128)(2,1)}, bf16[1024,1536]{1,0:T(8,128)(2,1)}...) custom-call(f32[8,1024]{1,0:T(8,128)} %maximum_maximum_fusion.tab_re, ...), custom_call_target="tpu_custom_call" | custom-call | tf_op jit(solution)/shard_map/pallas_call | solution.py:702
  300.9 1.2 slice.3
  302.8 0.0 copy-start.3
  302.8 3.2 %copy.21 = bf16[1,1024,1024]{2,1,0:T(8,128)(2,1)} copy(bf16[1,1024,1024]{2,1,0:T(8,128)(2,1)} %bitcast.24) | data formatting | bytes 4194304
  306.0 0.0 copy-done.3
  306.0 0.0 copy-start.2
  306.0 1.3 copy.22
  307.4 1.3 copy-done.2
  308.7 0.0 copy-start.1
  308.7 1.7 copy.23
  310.4 1.4 copy-done.1
  311.7 0.0 copy-start
  311.7 1.7 copy.24
  313.4 1.4 copy-done
  314.7 1.7 copy.25
  (2 shorter events, 0.0 us)
Async XLA Ops:
  302.8 3.2 %copy-start.3 = (bf16[1024,1024]{1,0:T(8,128)(2,1)S(1)}, bf16[1024,1024]{1,0:T(8,128)(2,1)}, u32[]{:S(2)}) copy-start(bf16[1024,1024]{1,0:T(8,128)(2,1)} %get-tuple-element.69) | copy-start | bytes 6291460
  306.0 2.6 copy-start.2
  308.7 3.0 copy-start.1
  311.7 3.0 copy-start
